TPU v7x, 256 devices: a whole 4x4x8 slice. The times are simulated.
256 devices in a mesh: time: 64 (over z_lo, y, x, core), chan: 4 (over z_hi).
Axes of the slice: x: 4, y: 4, z: 8 (z_hi: 4, z_lo: 2; z = z_hi * 2 + z_lo), core: 2. Of those that a mesh axis runs over, the one named last changes fastest.
Arguments:
- decay_rate: float32 [4, 32768, 2560], P(None, 'time', 'chan'), may hold values from 0.2 to 2
- drive_in: bfloat16 [4, 32768, 2560], P(None, 'time', 'chan'), may hold values from -6 to 6
- gate_in: bfloat16 [4, 32768, 2560], P(None, 'time', 'chan'), may hold values from -6 to 6
- norm_gain: float32 [2560], P('chan'), may hold values from 0.25 to 1.75
Outputs:
- filtered: bfloat16 [4, 32768, 2560], P(None, 'time', 'chan')
All inputs are finite; a program needn't handle non-finite values.
Results may differ from a plain program's by a relative error of at most 0.0015.
Values sent between devices are 32-bit elements.
A program may use at most 128 MiB of HBM per device.

v0:
```python
import jax
import jax.numpy as jnp
from jax import lax
from jax.sharding import Mesh
from jax.sharding import PartitionSpec as P

TIME = ("time_0", "time_1", "time_2", "time_3")


def nothing_yet(x, identity):
    return jax.tree.map(
        lambda part, zero: jnp.zeros_like(part) + jnp.asarray(zero, part.dtype), x, identity
    )


def entering(x, axes, combine, identity, reverse):
    before = start = nothing_yet(x, identity)
    so_far = x
    for axis in reversed(axes):
        peers, here = lax.axis_size(axis), lax.axis_index(axis)
        pieces = jax.tree.map(lambda part: lax.all_gather(part, axis), so_far)
        inside, so_far = start, start
        for k in reversed(range(peers)) if reverse else range(peers):
            passed = k > here if reverse else k < here
            so_far = combine(so_far, jax.tree.map(lambda part: part[k], pieces))
            inside = jax.tree.map(lambda new, old: jnp.where(passed, new, old), so_far, inside)
        before = combine(inside, before)
    return before


def gathered_total(x, axis):
    return lax.all_gather(x, axis).sum(0)


def join_pair(earlier, later):
    return (earlier[0] * later[0], later[0] * earlier[1] + later[1])


def body(decay_rate, drive_in, gate_in, norm_gain):
    total_length = decay_rate.shape[1] * lax.axis_size(TIME)
    keep = jnp.exp(-decay_rate / total_length)
    push = drive_in.astype(jnp.float32) * total_length ** (-0.5)
    steps = -decay_rate / total_length
    logs = jnp.sum(steps, axis=1, keepdims=True) - jnp.cumsum(steps, axis=1)
    summary = (jnp.exp(jnp.sum(steps, axis=1)), jnp.sum(jnp.exp(logs) * push, axis=1))
    entering_forward = entering(
        summary, TIME, join_pair, (jnp.ones_like(keep[:, 0]), jnp.zeros_like(push[:, 0])), False
    )
    started = push.at[:, 0].add(keep[:, 0] * entering_forward[1])
    forward = lax.associative_scan(join_pair, (keep, started), axis=1)[1]
    gated = forward * jax.nn.sigmoid(gate_in.astype(jnp.float32))
    power = gathered_total(jnp.sum(gated * gated, axis=-1, keepdims=True), "chan") / (
        gated.shape[-1] * lax.axis_size("chan")
    )
    filtered = (gated * lax.rsqrt(power + 1e-06) * norm_gain).astype(jnp.bfloat16)
    return filtered


def solution(mesh):
    split = Mesh(
        mesh.devices.reshape(2, 4, 4, 2, mesh.shape["chan"]),
        ("time_0", "time_1", "time_2", "time_3", "chan"),
    )
    in_specs = (P(None, TIME, "chan"), P(None, TIME, "chan"), P(None, TIME, "chan"), P("chan"))
    out_specs = P(None, TIME, "chan")
    return jax.shard_map(body, mesh=split, in_specs=in_specs, out_specs=out_specs, check_vma=False)
```

profile of v0, /device:TPU:32, one launch (start us, length us, event | category | flops | bytes accessed | tf_op | source)
XLA Modules:
  0.0 294.7 jit_solution(13377627184251010593)
XLA Ops:
  0.0 7.1 %fusion.24 = (f32[4,640]{1,0:T(4,128)S(1)}, f32[4,512,640]{2,1,0:T(8,128)}, f32[4,512,640]{2,1,0:T(8,128)}) fusion(f32[4,512,640]{2,1,0:T(8,128)} %param.6), kind=kLoop, calls=%fused_computation.120 | loop fusion | flops 3929600 | bytes 15738880 | tf_op jit(solution)/shard_map/reduce_sum | solution.py:45
  7.1 8.2 %fusion.2 = f32[4,640,4,128]{1,2,3,0:T(4,128)} fusion(f32[4,640,4,128]{1,3,2,0:T(8,128)} %bitcast.171), kind=kOutput, calls=%fused_computation.4 | output fusion | flops 166461440 | bytes 10485760 | tf_op jit(solution)/shard_map/reduce-window
  26.3 12.2 %all_gather.43 = f32[4,4,640]{2,1,0:T(4,128)S(1)} all-gather(f32[1,4,640]{2,1,0:T(4,128)S(1)} %copy.27), channel_id=1, replica_groups=mesh['time_0'=2,'time_1'=4,'time_2'=4,'time_3'=2,'chan'=4] {'time_2'}, dimensions={0}, use_global_device_ids=true | all-gather | bytes 51200 | tf_op jit(solution)/shard_map/all_gather | solution.py:21
  38.5 11.8 %all_gather.38 = f32[4,4,640]{2,1,0:T(4,128)S(1)} all-gather(f32[1,4,640]{2,1,0:T(4,128)S(1)} %copy.10), channel_id=1, replica_groups=mesh['time_0'=2,'time_1'=4,'time_2'=4,'time_3'=2,'chan'=4] {'time_2'}, dimensions={0}, use_global_device_ids=true | all-gather | bytes 51200 | tf_op jit(solution)/shard_map/all_gather | solution.py:21
  50.4 12.4 %all_gather.44 = f32[4,4,640]{2,1,0:T(4,128)S(1)} all-gather(f32[1,4,640]{2,1,0:T(4,128)S(1)} %copy.32), channel_id=1, replica_groups=mesh['time_0'=2,'time_1'=4,'time_2'=4,'time_3'=2,'chan'=4] {'time_1'}, dimensions={0}, use_global_device_ids=true | all-gather | bytes 51200 | tf_op jit(solution)/shard_map/all_gather | solution.py:21
  62.8 11.8 %all_gather.39 = f32[4,4,640]{2,1,0:T(4,128)S(1)} all-gather(f32[1,4,640]{2,1,0:T(4,128)S(1)} %copy.15), channel_id=1, replica_groups=mesh['time_0'=2,'time_1'=4,'time_2'=4,'time_3'=2,'chan'=4] {'time_1'}, dimensions={0}, use_global_device_ids=true | all-gather | bytes 51200 | tf_op jit(solution)/shard_map/all_gather | solution.py:21
  74.7 4.4 %all_gather.40 = f32[2,4,640]{2,1,0:T(4,128)S(1)} all-gather(f32[1,4,640]{2,1,0:T(4,128)S(1)} %copy.20), channel_id=1, replica_groups=mesh['time_0'=2,'time_1'=4,'time_2'=4,'time_3'=2,'chan'=4] {'time_0'}, dimensions={0}, use_global_device_ids=true | all-gather | bytes 30720 | tf_op jit(solution)/shard_map/all_gather | solution.py:21
  79.0 4.5 %all_gather.45 = f32[2,4,640]{2,1,0:T(4,128)S(1)} all-gather(f32[1,4,640]{2,1,0:T(4,128)S(1)} %copy.37), channel_id=1, replica_groups=mesh['time_0'=2,'time_1'=4,'time_2'=4,'time_3'=2,'chan'=4] {'time_0'}, dimensions={0}, use_global_device_ids=true | all-gather | bytes 30720 | tf_op jit(solution)/shard_map/all_gather | solution.py:21
  86.2 14.1 %slice.401 = f32[4,255,640]{2,1,0:T(8,128)} slice(f32[4,512,640]{2,1,0:T(8,128)} %scatter-add.4), slice={[0:4:1], [2:512:2], [0:640:1]} | slice | bytes 5222400 | tf_op jit(solution)/shard_map/slice | solution.py:50
  100.3 14.0 %slice.339 = f32[4,256,640]{2,1,0:T(8,128)} slice(f32[4,512,640]{2,1,0:T(8,128)} %scatter-add.4), slice={[0:4:1], [1:512:2], [0:640:1]} | slice | bytes 5242880 | tf_op jit(solution)/shard_map/slice | solution.py:50
  114.3 14.0 %slice.338 = f32[4,256,640]{2,1,0:T(8,128)} slice(f32[4,512,640]{2,1,0:T(8,128)} %scatter-add.4), slice={[0:4:1], [0:511:2], [0:640:1]} | slice | bytes 5242880 | tf_op jit(solution)/shard_map/slice | solution.py:50
  128.3 14.0 %slice.341 = f32[4,256,640]{2,1,0:T(8,128)} slice(f32[4,512,640]{2,1,0:T(8,128)} %get-tuple-element.20), slice={[0:4:1], [0:511:2], [0:640:1]} | slice | bytes 5242880 | tf_op jit(solution)/shard_map/slice | solution.py:50
  142.3 14.0 %slice.337 = f32[4,256,640]{2,1,0:T(8,128)} slice(f32[4,512,640]{2,1,0:T(8,128)} %get-tuple-element.20), slice={[0:4:1], [1:512:2], [0:640:1]} | slice | bytes 5242880 | tf_op jit(solution)/shard_map/slice | solution.py:50
  156.3 6.1 %fusion.26 = (f32[4,256,640]{2,1,0:T(8,128)}, f32[4,256,640]{2,1,0:T(8,128)S(1)}) fusion(f32[4,256,640]{2,1,0:T(8,128)} %slice.341, f32[4,256,640]{2,1,0:T(8,128)} %slice.337, f32[4,256,640]{2,1,0:T(8,128)} %slice.339, f32[4,256,640]{2,1,0:T(8,128)} %slice.338), kind=kLoop, calls=%fused_computation.122 | loop fusion | flops 1966080 | bytes 15728640 | tf_op jit(solution)/shard_map/mul | solution.py:36
  162.4 14.1 %slice.336 = f32[4,255,640]{2,1,0:T(8,128)} slice(f32[4,512,640]{2,1,0:T(8,128)} %get-tuple-element.20), slice={[0:4:1], [2:512:2], [0:640:1]} | slice | bytes 5222400 | tf_op jit(solution)/shard_map/slice | solution.py:50
  176.5 7.5 %slice.347 = f32[4,128,640]{2,1,0:T(8,128)} slice(f32[4,256,640]{2,1,0:T(8,128)} %get-tuple-element.22), slice={[0:4:1], [0:255:2], [0:640:1]} | slice | bytes 2621440 | tf_op jit(solution)/shard_map/slice | solution.py:50
  184.0 7.5 %slice.343 = f32[4,128,640]{2,1,0:T(8,128)} slice(f32[4,256,640]{2,1,0:T(8,128)} %get-tuple-element.22), slice={[0:4:1], [1:256:2], [0:640:1]} | slice | bytes 2621440 | tf_op jit(solution)/shard_map/slice | solution.py:50
  191.5 7.6 %slice.342 = f32[4,127,640]{2,1,0:T(8,128)} slice(f32[4,256,640]{2,1,0:T(8,128)} %get-tuple-element.22), slice={[0:4:1], [2:256:2], [0:640:1]} | slice | bytes 2600960 | tf_op jit(solution)/shard_map/slice | solution.py:50
  238.9 5.4 %pad.72 = f32[4,256,640]{2,1,0:T(8,128)} pad(f32[4,128,640]{2,1,0:T(8,128)} %add.337, f32[]{:T(128)} %constant.61.clone.1), padding=0_0_0x1_0_1x0_0_0 | pad | bytes 3932164 | tf_op jit(solution)/shard_map/pad | solution.py:50
  250.5 6.6 %pad.73 = f32[4,512,640]{2,1,0:T(8,128)} pad(f32[4,256,640]{2,1,0:T(8,128)S(1)} %pad_maximum_fusion, f32[]{:T(128)} %constant.61.clone.1), padding=0_0_0x0_1_1x0_0_0 | pad | bytes 7864324 | tf_op jit(solution)/shard_map/pad | solution.py:50
  257.1 10.3 %pad.74 = f32[4,512,640]{2,1,0:T(8,128)} pad(f32[4,256,640]{2,1,0:T(8,128)} %add.339, f32[]{:T(128)} %constant.61.clone.1), padding=0_0_0x1_0_1x0_0_0 | pad | bytes 7864324 | tf_op jit(solution)/shard_map/pad | solution.py:50
  267.4 6.4 %multiply_reduce_fusion = (f32[4,512]{1,0:T(4,128)S(1)}, f32[4,512,640]{2,1,0:T(8,128)}) fusion(bf16[4,512,640]{2,1,0:T(8,128)(2,1)S(1)} %copy-done.4, f32[4,512,640]{2,1,0:T(8,128)} %pad.73, f32[4,512,640]{2,1,0:T(8,128)} %pad.74), kind=kLoop, calls=%fused_computation.7 | loop fusion | flops 10483712 | bytes 18358272 | tf_op jit(solution)/shard_map/reduce_sum | solution.py:52
  273.8 16.3 %all-gather.5 = f32[4,4,512]{2,1,0:T(4,128)S(1)} all-gather(f32[1,4,512]{2,1,0:T(4,128)S(1)} %bitcast.187), channel_id=4, replica_groups=mesh['time_0'=2,'time_1'=4,'time_2'=4,'time_3'=2,'chan'=4] {'chan'}, dimensions={0}, use_global_device_ids=true | all-gather | bytes 40960 | tf_op jit(solution)/shard_map/all_gather | solution.py:32
  290.2 4.5 %multiply_convert_fusion = bf16[4,512,640]{2,1,0:T(8,128)(2,1)} fusion(f32[4,512,640]{2,1,0:T(8,128)} %get-tuple-element.18, f32[640]{0:T(1024)S(1)} %copy-done.6, f32[4,512]{1,0:T(4,128)S(1)} %add_rsqrt_fusion), kind=kLoop, calls=%fused_computation.6 | loop fusion | flops 3932160 | bytes 7875072 | tf_op jit(solution)/shard_map/convert_element_type | solution.py:55
  (132 shorter events, 59.3 us)
Async XLA Ops:
  21.5 1.7 copy-start.2
  24.4 59.2 %copy-start = (f32[4,512,640]{2,1,0:T(8,128)}, f32[4,512,640]{2,1,0:T(8,128)S(1)}, u32[]{:S(2)}) copy-start(f32[4,512,640]{2,1,0:T(8,128)S(1)} %get-tuple-element.25) | copy-start | bytes 15728644
  218.3 3.5 %copy-start.3 = (f32[4,64,640]{2,1,0:T(8,128)S(1)}, f32[4,64,640]{2,1,0:T(8,128)}, u32[]{:S(2)}) copy-start(f32[4,64,640]{2,1,0:T(8,128)} %slice.353) | copy-start | bytes 1966084
  229.7 1.1 copy-start.5
  244.3 4.0 %copy-start.1 = (f32[4,256,640]{2,1,0:T(8,128)S(1)}, f32[4,256,640]{2,1,0:T(8,128)}, u32[]{:S(2)}) copy-start(f32[4,256,640]{2,1,0:T(8,128)} %pad.72) | copy-start | bytes 7864324
  257.1 10.3 %copy-start.4 = (bf16[4,512,640]{2,1,0:T(8,128)(2,1)S(1)}, bf16[4,512,640]{2,1,0:T(8,128)(2,1)}, u32[]{:S(2)}) copy-start(bf16[4,512,640]{2,1,0:T(8,128)(2,1)} %param.8) | copy-start | bytes 7864324
  267.4 22.8 %copy-start.6 = (f32[640]{0:T(1024)S(1)}, f32[640]{0:T(1024)}, u32[]{:S(2)}) copy-start(f32[640]{0:T(1024)} %param.9) | copy-start | bytes 7684
where the time goes:
time: 299 us; the launch traced here: 295 us
  local copies, waits for them, and re-layouts  162 us (54%)
  blocking collectives  77 us (26%)
  other arithmetic  55.2 us (18%)
    slice x52, local copies, waits for them, and re-layouts, body(): forward = lax.associative_scan(join_pair, (keep, started), axis=1)[1]  132 us
    all_gather x8, blocking collectives, entering(): pieces = jax.tree.map(lambda part: lax.all_gather(part, axis), so_far)  60.7 us
    pad x16, local copies, waits for them, and re-layouts, body(): forward = lax.associative_scan(join_pair, (keep, started), axis=1)[1]  26.1 us
    all_gather x1, blocking collectives, gathered_total(): return lax.all_gather(x, axis).sum(0)  16.3 us
    mul x10, other arithmetic, join_pair(): return (earlier[0] * later[0], later[0] * earlier[1] + later[1])  12 us
    another operation x3, other arithmetic  11.7 us
    reduce_sum x1, other arithmetic, body(): jnp.sum(steps, axis=1)  7.13 us
    reduce_sum x1, other arithmetic, body(): jnp.sum(gated * gated, axis=-1, keepdims=True)  6.4 us

commit v1 on v0

v1 whole, which is shorter than its diff:
```python
import functools
import math

import jax
import jax.numpy as jnp
from jax import lax
from jax.experimental import pallas as pl
from jax.experimental.pallas import tpu as pltpu
from jax.sharding import PartitionSpec as P

MESH = pl.DeviceIdType.MESH
BLOCK = 256
LANES = 128
CHUNK = 16
COLS = 8
F32 = jnp.float32
BF16 = jnp.bfloat16
NT = (((1,), (1,)), ((), ()))
TN = (((0,), (0,)), ((), ()))


def iota(shape, dim):
    return lax.broadcasted_iota(jnp.int32, shape, dim)


def triangle(width):
    row, column = iota((BLOCK, width), 0), iota((BLOCK, width), 1)
    return jnp.where(lax.rem(column, BLOCK) <= row, 1.0, 0.0).astype(BF16)


def by_rows(x):
    return x.reshape(x.shape[0] // 8, 8, x.shape[1]).sum(0)


def state_kernel(
    times, chans, decay_hbm, drive_hbm, gate_hbm, gated_ref, scale_ref,
    decay, drives, gate, logs, local, squares, ends, row_buf, col_buf, power_buf,
    decay_sem, drive_sem, gate_sem, row_send, row_recv, col_send, col_recv, power_send, power_recv,
):
    batch, length, width = decay_hbm.shape
    halves = length // BLOCK
    blocks = batch * halves
    rows = times // COLS
    total_length = length * times
    log2_scale = math.log2(math.e) / total_length
    time, chan = lax.axis_index("time"), lax.axis_index("chan")
    row, col = time // COLS, lax.rem(time, COLS)

    def at(ref, block):
        return ref.at[block // halves, pl.ds(block % halves * BLOCK, BLOCK), :]

    loads = {}
    for block in range(blocks):
        loads["decay", block] = pltpu.make_async_copy(at(decay_hbm, block), decay.at[block], decay_sem.at[block])
        loads["drive", block] = pltpu.make_async_copy(at(drive_hbm, block), drives.at[block, 0], drive_sem.at[block])
        loads["gate", block] = pltpu.make_async_copy(at(gate_hbm, block), gate.at[block], gate_sem.at[block])
    for block in range(blocks):
        loads["decay", block].start()
        loads["drive", block].start()
    for block in range(blocks):
        loads["gate", block].start()

    row_peers = [(row * COLS + lax.rem(col + k, COLS), chan) for k in range(1, COLS)]
    col_peers = [(lax.rem(row + k, rows) * COLS + col, chan) for k in range(1, rows)]
    chan_peers = [(time, lax.rem(chan + k, chans)) for k in range(1, chans)]
    barrier = pltpu.get_barrier_semaphore()
    for peer in row_peers + col_peers + chan_peers:
        pl.semaphore_signal(barrier, inc=1, device_id=peer, device_id_type=MESH)

    lower = triangle(BLOCK)
    both = triangle(2 * BLOCK)

    for block in range(blocks):
        loads["decay", block].wait()
        logs[block] = jnp.dot(lower, decay[block].astype(BF16), preferred_element_type=F32)
        loads["drive", block].wait()

        def step(i, carry):
            drive_sum, decay_sum = carry
            here = pl.ds(pl.multiple_of(i * CHUNK, CHUNK), CHUNK)
            drive = drives[block, 0, here, :].astype(F32)
            grown = drive * jnp.exp2(logs[block, here, :] * log2_scale)
            drives[block, 1, here, :] = (grown - drive).astype(BF16)
            return drive_sum + by_rows(grown), decay_sum + by_rows(decay[block, here, :])

        zero = jnp.zeros((8, width), F32)
        drive_sum, decay_sum = lax.fori_loop(0, BLOCK // CHUNK, step, (zero, zero), unroll=2)
        shrink = jnp.exp2(decay_sum.sum(0, keepdims=True) * -log2_scale)
        ends[block : block + 1, :] = shrink
        ends[blocks + block : blocks + block + 1, :] = shrink * drive_sum.sum(0, keepdims=True)

    for b in range(batch):
        keep, state = jnp.ones((1, width), F32), jnp.zeros((1, width), F32)
        for block in range(b * halves, (b + 1) * halves):
            shrink = ends[block : block + 1, :]
            keep, state = keep * shrink, shrink * state + ends[blocks + block : blocks + block + 1, :]
        row_buf[col, b : b + 1, :] = keep
        row_buf[col, batch + b : batch + b + 1, :] = state

    pl.semaphore_wait(barrier, len(row_peers + col_peers + chan_peers))
    row_copies = [
        pltpu.make_async_remote_copy(
            row_buf.at[col], row_buf.at[col], row_send.at[k], row_recv.at[col], device_id=peer, device_id_type=MESH
        )
        for k, peer in enumerate(row_peers)
    ]
    for copy in row_copies:
        copy.start()

    def gate_block(block):
        stacked = drives[block].reshape(2 * BLOCK, width)
        local[block] = jnp.dot(both, stacked, preferred_element_type=F32)
        loads["gate", block].wait()

        def step(i, carry):
            here = pl.ds(pl.multiple_of(i * CHUNK, CHUNK), CHUNK)
            half = 0.5 * total_length**-0.5
            sigmoid = jnp.tanh(gate[block, here, :].astype(F32) * 0.5) * half + half
            logs[block, here, :] = jnp.exp2(logs[block, here, :] * -log2_scale) * sigmoid
            return carry

        lax.fori_loop(0, BLOCK // CHUNK, step, 0, unroll=2)

    for block in range(blocks // 2):
        gate_block(block)

    for k in range(1, COLS):
        source = lax.rem(col + k, COLS)
        pltpu.make_async_remote_copy(
            row_buf.at[source], row_buf.at[source], row_send.at[k - 1], row_recv.at[source],
            device_id=(time, chan), device_id_type=MESH,
        ).wait_recv()
    keep, state = jnp.ones((batch, width), F32), jnp.zeros((batch, width), F32)
    keep_before, state_before = keep, state
    for j in range(COLS):
        a, b = row_buf[j, :batch, :], row_buf[j, batch:, :]
        keep, state = a * keep, a * state + b
        passed = j < col
        keep_before, state_before = jnp.where(passed, keep, keep_before), jnp.where(passed, state, state_before)
    col_buf[row, :batch, :] = keep
    col_buf[row, batch:, :] = state
    col_copies = []
    for k in range(1, rows):
        copy = pltpu.make_async_remote_copy(
            col_buf.at[row], col_buf.at[row], col_send.at[k - 1], col_recv.at[row],
            device_id=(lax.rem(row + k, rows) * COLS + col, chan), device_id_type=MESH,
        )
        col_copies.append(copy)
        pl.when(row + k < rows)(copy.start)

    for block in range(blocks // 2, blocks):
        gate_block(block)

    for k in range(1, rows):
        source = lax.rem(row + k, rows)
        copy = pltpu.make_async_remote_copy(
            col_buf.at[source], col_buf.at[source], col_send.at[k - 1], col_recv.at[source],
            device_id=(time, chan), device_id_type=MESH,
        )
        pl.when(source < row)(copy.wait_recv)
    entering = jnp.zeros((batch, width), F32)
    for j in range(rows):
        new = col_buf[j, :batch, :] * entering + col_buf[j, batch:, :]
        entering = jnp.where(j < row, new, entering)
    entering = keep_before * entering + state_before

    powers = jnp.zeros((blocks, BLOCK), F32)
    for b in range(batch):
        start = entering[b : b + 1, :]
        for block in range(b * halves, (b + 1) * halves):
            where = block % halves * BLOCK

            def step(i, carry):
                here = pl.ds(pl.multiple_of(i * CHUNK, CHUNK), CHUNK)
                there = pl.ds(pl.multiple_of(where + i * CHUNK, CHUNK), CHUNK)
                gated = logs[block, here, :] * (local[block, here, :] + start)
                gated_ref[b, there, :] = gated
                square = gated * gated
                squares[here, :] = sum(square[:, k : k + LANES] for k in range(0, width, LANES))
                return carry

            lax.fori_loop(0, BLOCK // CHUNK, step, 0, unroll=2)
            high = squares[...].astype(BF16)
            rest = (squares[...] - high.astype(F32)).astype(BF16)
            pick = jnp.where(iota((blocks, 2 * LANES), 0) == block, 1.0, 0.0).astype(BF16)
            powers = powers + lax.dot_general(
                pick, jnp.concatenate([high, rest], axis=1), NT, preferred_element_type=F32
            )
            if block + 1 < (b + 1) * halves:
                start = ends[block : block + 1, :] * (local[block, BLOCK - 1 :, :] + start)
    power_buf[chan] = powers
    power_copies = [
        pltpu.make_async_remote_copy(
            power_buf.at[chan], power_buf.at[chan], power_send.at[k], power_recv.at[chan],
            device_id=peer, device_id_type=MESH,
        )
        for k, peer in enumerate(chan_peers)
    ]
    for copy in power_copies:
        copy.start()
    for k in range(1, chans):
        source = lax.rem(chan + k, chans)
        pltpu.make_async_remote_copy(
            power_buf.at[source], power_buf.at[source], power_send.at[k - 1], power_recv.at[source],
            device_id=(time, chan), device_id_type=MESH,
        ).wait_recv()
    power = sum(power_buf[j] for j in range(chans)) / (width * chans)
    scale_ref[...] = lax.rsqrt(power + 1e-06)

    for copy in row_copies + power_copies:
        copy.wait_send()
    for k, copy in enumerate(col_copies):
        pl.when(row + k + 1 < rows)(copy.wait_send)


def scale_kernel(gated_ref, scale_ref, gain_ref, out_ref):
    block = pl.program_id(0) * pl.num_programs(1) + pl.program_id(1)
    blocks = scale_ref.shape[0]
    pick = jnp.where(iota((blocks, LANES), 0) == block, 1.0, 0.0)
    scale = lax.dot_general(scale_ref[...], pick, TN, precision=lax.Precision.HIGHEST, preferred_element_type=F32)
    for k in range(0, out_ref.shape[-1], LANES):
        lane = slice(k, k + LANES)
        out_ref[0, :, lane] = (gated_ref[0, :, lane] * scale * gain_ref[:, lane]).astype(out_ref.dtype)


def solution(mesh):
    times, chans = mesh.shape["time"], mesh.shape["chan"]

    def body(decay_rate, drive_in, gate_in, norm_gain):
        batch, length, width = decay_rate.shape
        halves = length // BLOCK
        blocks = batch * halves
        rows = times // COLS
        dma = pltpu.SemaphoreType.DMA
        gated, scale = pl.pallas_call(
            functools.partial(state_kernel, times, chans),
            out_shape=(pltpu.VMEM((batch, length, width), F32), pltpu.VMEM((blocks, BLOCK), F32)),
            in_specs=[pl.BlockSpec(memory_space=pltpu.HBM)] * 3,
            out_specs=(pl.BlockSpec(memory_space=pltpu.VMEM), pl.BlockSpec(memory_space=pltpu.VMEM)),
            scratch_shapes=[
                pltpu.VMEM((blocks, BLOCK, width), F32),
                pltpu.VMEM((blocks, 2, BLOCK, width), BF16),
                pltpu.VMEM((blocks, BLOCK, width), BF16),
                pltpu.VMEM((blocks, BLOCK, width), F32),
                pltpu.VMEM((blocks, BLOCK, width), F32),
                pltpu.VMEM((BLOCK, LANES), F32),
                pltpu.VMEM((2 * blocks, width), F32),
                pltpu.VMEM((COLS, 2 * batch, width), F32),
                pltpu.VMEM((rows, 2 * batch, width), F32),
                pltpu.VMEM((chans, blocks, BLOCK), F32),
                dma((blocks,)), dma((blocks,)), dma((blocks,)),
                dma((COLS - 1,)), dma((COLS,)),
                dma((rows - 1,)), dma((rows,)),
                dma((chans - 1,)), dma((chans,)),
            ],
            compiler_params=pltpu.CompilerParams(
                collective_id=0, has_side_effects=True, vmem_limit_bytes=40 * 2**20
            ),
        )(decay_rate, drive_in, gate_in)
        return pl.pallas_call(
            scale_kernel,
            out_shape=jax.ShapeDtypeStruct((batch, length, width), BF16),
            grid=(batch, halves),
            in_specs=[
                pl.BlockSpec((1, BLOCK, width), lambda b, h: (b, h, 0)),
                pl.BlockSpec((blocks, BLOCK), lambda b, h: (0, 0)),
                pl.BlockSpec((1, width), lambda b, h: (0, 0)),
            ],
            out_specs=pl.BlockSpec((1, BLOCK, width), lambda b, h: (b, h, 0)),
            compiler_params=pltpu.CompilerParams(vmem_limit_bytes=16 * 2**20),
        )(gated, scale, norm_gain.reshape(1, width))

    in_specs = (P(None, "time", "chan"), P(None, "time", "chan"), P(None, "time", "chan"), P("chan"))
    return jax.shard_map(body, mesh=mesh, in_specs=in_specs, out_specs=P(None, "time", "chan"), check_vma=False)
```

time: 299 us -> 37 us (0.12); the launches traced: 295 us -> 36.8 us
  local copies, waits for them, and re-layouts: 162 us -> 4.17 us
  blocking collectives: 77 us -> 0 us
  other arithmetic: 55.2 us -> 0 us
  Pallas kernels: 0 us -> 32.6 us
    slice x60 -> x0, local copies, waits for them, and re-layouts: 132 us -> none  [the longest x52 132 us: body(): forward = lax.associative_scan(join_pair, (keep, started), axis=1)[1]]
    all_gather x9 -> x0, blocking collectives: 77 us -> none  [the longest x8 60.7 us: entering(): pieces = jax.tree.map(lambda part: lax.all_gather(part, axis), so_far)]
    pallas_call x0 -> x2, Pallas kernels: none -> 32.6 us  [the longest x1 27.9 us: body(): pl.pallas_call(functools.partial(state_kernel, times, chans), out_shape=(...]
    pad x16 -> x0, local copies, waits for them, and re-layouts: 26.1 us -> none  [body(): forward = lax.associative_scan(join_pair, (keep, started), axis=1)[1]]
    reduce_sum x4 -> x0, other arithmetic: 14.8 us -> none  [the longest x1 7.13 us: body(): jnp.sum(steps, axis=1)]
    mul x10 -> x0, other arithmetic: 12 us -> none  [join_pair(): return (earlier[0] * later[0], later[0] * earlier[1] + later[1])]
    another operation x3 -> x0, other arithmetic: 11.7 us -> none
    add x18 -> x0, other arithmetic: 10.6 us -> none  [the longest x9 6.21 us: join_pair(): return (earlier[0] * later[0], later[0] * earlier[1] + later[1])]
where the time goes in v1:
time: 37 us; the launch traced here: 36.8 us
  Pallas kernels  32.6 us (88%)
  local copies, waits for them, and re-layouts  4.17 us (11%)
    pallas_call x1, Pallas kernels, body(): pl.pallas_call(functools.partial(state_kernel, times, chans), out_shape=(...  27.9 us
    pallas_call x1, Pallas kernels, body(): pl.pallas_call(scale_kernel, out_shape=jax.ShapeDtypeStruct((batch, lengt...  4.79 us
    unnamed x4, local copies, waits for them, and re-layouts  3.48 us

profile of v1, /device:TPU:32, one launch (start us, length us, event | category | flops | bytes accessed | tf_op | source)
XLA Modules:
  0.0 36.8 jit_solution(14659512146210341358)
XLA Ops:
  0.0 0.7 %reshape.3.gain_ref = f32[1,640]{1,0:T(1,128)S(1)} reshape(f32[640]{0:T(1024)} %param.7) | data formatting | bytes 5120 | tf_op jit(solution)/shard_map/reshape | solution.py:271
  0.7 0.0 copy-start
  0.7 1.7 %copy-done = bf16[4,512,640]{2,1,0:T(8,128)(2,1)S(1)} copy-done((bf16[4,512,640]{2,1,0:T(8,128)(2,1)S(1)}, bf16[4,512,640]{2,1,0:T(8,128)(2,1)}, u32[]{:S(2)}) %copy-start) | copy-done | bytes 2621464
  2.4 0.0 copy-start.1
  2.4 1.7 %copy-done.1 = bf16[4,512,640]{2,1,0:T(8,128)(2,1)S(1)} copy-done((bf16[4,512,640]{2,1,0:T(8,128)(2,1)S(1)}, bf16[4,512,640]{2,1,0:T(8,128)(2,1)}, u32[]{:S(2)}) %copy-start.1) | copy-done | bytes 2621464
  4.2 27.9 %shard_map.46 = (f32[4,512,640]{2,1,0:T(8,128)S(1)}, f32[8,256]{1,0:T(8,128)S(1)}) custom-call(f32[4,512,640]{2,1,0:T(8,128)} %decay_hbm.1, bf16[4,512,640]{2,1,0:T(8,128)(2,1)S(1)} %copy-done, bf16[4,512,640]{2,1,0:T(8,128)(2,1)S(1)} %copy-done.1), custom_call_target="tpu_custom_call" | custom-call | tf_op jit(solution)/shard_map/pallas_call | solution.py:235
  32.0 4.8 %shard_map.47 = bf16[4,512,640]{2,1,0:T(8,128)(2,1)} custom-call(f32[4,512,640]{2,1,0:T(8,128)S(1)} %get-tuple-element.7.gated_ref, f32[8,256]{1,0:T(8,128)S(1)} %get-tuple-element.8.scale_ref, f32[1,640]{1,0:T(1,128)S(1)} %reshape.3.gain_ref), custom_call_target="tpu_custom_call" | custom-call | tf_op jit(solution)/shard_map/pallas_call | solution.py:260
Async XLA Ops:
  0.7 1.7 %copy-start = (bf16[4,512,640]{2,1,0:T(8,128)(2,1)S(1)}, bf16[4,512,640]{2,1,0:T(8,128)(2,1)}, u32[]{:S(2)}) copy-start(bf16[4,512,640]{2,1,0:T(8,128)(2,1)} %drive_hbm.1) | copy-start | bytes 7864324
  2.4 1.7 %copy-start.1 = (bf16[4,512,640]{2,1,0:T(8,128)(2,1)S(1)}, bf16[4,512,640]{2,1,0:T(8,128)(2,1)}, u32[]{:S(2)}) copy-start(bf16[4,512,640]{2,1,0:T(8,128)(2,1)} %gate_hbm.1) | copy-start | bytes 7864324

commit v2 on v1

--- a/solution.py
+++ b/solution.py
@@ -215,12 +215,18 @@
 
 def scale_kernel(gated_ref, scale_ref, gain_ref, out_ref):
     block = pl.program_id(0) * pl.num_programs(1) + pl.program_id(1)
-    blocks = scale_ref.shape[0]
-    pick = jnp.where(iota((blocks, LANES), 0) == block, 1.0, 0.0)
-    scale = lax.dot_general(scale_ref[...], pick, TN, precision=lax.Precision.HIGHEST, preferred_element_type=F32)
+    scale = scale_ref[pl.ds(block, 1), :]
+    high = scale.astype(BF16)
+    rest = (scale - high.astype(F32)).astype(BF16)
+    square = (BLOCK, BLOCK)
+    diagonal = iota(square, 0) == iota(square, 1)
+    spread = [jnp.where(diagonal, jnp.broadcast_to(part.astype(F32), square), 0.0).astype(BF16) for part in (high, rest)]
+    ones = jnp.ones((2 * BLOCK, LANES), BF16)
+    scale = jnp.dot(jnp.concatenate(spread, axis=1), ones, preferred_element_type=F32)
     for k in range(0, out_ref.shape[-1], LANES):
         lane = slice(k, k + LANES)
-        out_ref[0, :, lane] = (gated_ref[0, :, lane] * scale * gain_ref[:, lane]).astype(out_ref.dtype)
+        gain = gain_ref[lane].reshape(1, LANES)
+        out_ref[0, :, lane] = (gated_ref[0, :, lane] * scale * gain).astype(out_ref.dtype)
 
 
 def solution(mesh):
@@ -254,7 +260,7 @@
                 dma((chans - 1,)), dma((chans,)),
             ],
             compiler_params=pltpu.CompilerParams(
-                collective_id=0, has_side_effects=True, vmem_limit_bytes=40 * 2**20
+                collective_id=0, has_side_effects=True, vmem_limit_bytes=57 * 2**20
             ),
         )(decay_rate, drive_in, gate_in)
         return pl.pallas_call(
@@ -264,11 +270,11 @@
             in_specs=[
                 pl.BlockSpec((1, BLOCK, width), lambda b, h: (b, h, 0)),
                 pl.BlockSpec((blocks, BLOCK), lambda b, h: (0, 0)),
-                pl.BlockSpec((1, width), lambda b, h: (0, 0)),
+                pl.BlockSpec((width,), lambda b, h: (0,)),
             ],
             out_specs=pl.BlockSpec((1, BLOCK, width), lambda b, h: (b, h, 0)),
             compiler_params=pltpu.CompilerParams(vmem_limit_bytes=16 * 2**20),
-        )(gated, scale, norm_gain.reshape(1, width))
+        )(gated, scale, norm_gain)
 
     in_specs = (P(None, "time", "chan"), P(None, "time", "chan"), P(None, "time", "chan"), P("chan"))
     return jax.shard_map(body, mesh=mesh, in_specs=in_specs, out_specs=P(None, "time", "chan"), check_vma=False)

time: 37 us -> 31.3 us (0.85)
  local copies, waits for them, and re-layouts: 4.17 us -> 0.01 us
  Pallas kernels: 32.6 us -> 31.2 us
    unnamed x4 -> x2, local copies, waits for them, and re-layouts: 3.48 us -> 0.01 us
    pallas_call x1, Pallas kernels: 27.9 us -> 27.1 us  [body(): pl.pallas_call(functools.partial(state_kernel, times, chans), out_shape=(...]
    reshape x1 -> x0, local copies, waits for them, and re-layouts: 0.69 us -> none  [body(): norm_gain.reshape(1, width)]
    pallas_call x1, Pallas kernels: 4.79 us -> 4.11 us  [body(): pl.pallas_call(scale_kernel, out_shape=jax.ShapeDtypeStruct((batch, lengt...]
where the time goes in v2:
time: 31.3 us; the launch traced here: 31.2 us
  Pallas kernels  31.2 us (100%)
    pallas_call x1, Pallas kernels, body(): pl.pallas_call(functools.partial(state_kernel, times, chans), out_shape=(...  27.1 us
    pallas_call x1, Pallas kernels, body(): pl.pallas_call(scale_kernel, out_shape=jax.ShapeDtypeStruct((batch, lengt...  4.11 us

profile of v2, /device:TPU:32, one launch (start us, length us, event | category | flops | bytes accessed | tf_op | source)
XLA Modules:
  0.0 31.2 jit_solution(17106103806594226539)
XLA Ops:
  0.0 0.0 copy-start
  0.0 27.1 %shard_map.46 = (f32[4,512,640]{2,1,0:T(8,128)S(1)}, f32[8,256]{1,0:T(8,128)S(1)}) custom-call(f32[4,512,640]{2,1,0:T(8,128)} %decay_hbm.1, bf16[4,512,640]{2,1,0:T(8,128)(2,1)} %drive_hbm.1, bf16[4,512,640]{2,1,0:T(8,128)(2,1)} %gate_hbm.1), custom_call_target="tpu_custom_call" | custom-call | tf_op jit(solution)/shard_map/pallas_call | solution.py:241
  27.1 0.0 copy-done
  27.1 4.1 %shard_map.47 = bf16[4,512,640]{2,1,0:T(8,128)(2,1)} custom-call(f32[4,512,640]{2,1,0:T(8,128)S(1)} %get-tuple-element.7.gated_ref, f32[8,256]{1,0:T(8,128)S(1)} %get-tuple-element.8.scale_ref, f32[640]{0:T(1024)S(1)} %copy-done), custom_call_target="tpu_custom_call" | custom-call | tf_op jit(solution)/shard_map/pallas_call | solution.py:266
Async XLA Ops:
  0.0 27.1 %copy-start = (f32[640]{0:T(1024)S(1)}, f32[640]{0:T(1024)}, u32[]{:S(2)}) copy-start(f32[640]{0:T(1024)} %gain_ref.1) | copy-start | bytes 7684

commit v3 on v1

v3 whole, which is shorter than its diff:
```python
import functools
import math

import jax
import jax.numpy as jnp
from jax import lax
from jax.experimental import pallas as pl
from jax.experimental.pallas import tpu as pltpu
from jax.sharding import PartitionSpec as P

MESH = pl.DeviceIdType.MESH
BLOCK = 256
LANES = 128
CHUNK = 16
COLS = 8
F32 = jnp.float32
BF16 = jnp.bfloat16
NT = (((1,), (1,)), ((), ()))
TN = (((0,), (0,)), ((), ()))


def iota(shape, dim):
    return lax.broadcasted_iota(jnp.int32, shape, dim)


def triangle(width):
    row, column = iota((BLOCK, width), 0), iota((BLOCK, width), 1)
    return jnp.where(lax.rem(column, BLOCK) <= row, 1.0, 0.0).astype(BF16)


def parts(x):
    high = x.astype(BF16)
    return high, (x - high.astype(F32)).astype(BF16)


def state_kernel(
    times, chans, decay_hbm, drive_hbm, gate_hbm, gated_ref, scale_ref,
    decay, drives, gate, logs, local, rounded, lower, ends, row_buf, col_buf, power_buf,
    decay_sem, drive_sem, row_send, row_recv, col_send, col_recv, power_send, power_recv,
):
    batch, length, width = decay_hbm.shape
    halves = length // BLOCK
    blocks = batch * halves
    rows = times // COLS
    total_length = length * times
    log2_scale = math.log2(math.e) / total_length
    time, chan = lax.axis_index("time"), lax.axis_index("chan")
    row, col = time // COLS, lax.rem(time, COLS)

    def at(ref, block):
        return ref.at[block // halves, pl.ds(block % halves * BLOCK, BLOCK), :]

    decays = [pltpu.make_async_copy(at(decay_hbm, k), decay.at[k], decay_sem.at[k]) for k in range(blocks)]
    driving = [pltpu.make_async_copy(at(drive_hbm, k), drives.at[k, 0], drive_sem.at[k]) for k in range(blocks)]
    gates = [pltpu.make_async_copy(at(gate_hbm, k), gate.at[k], decay_sem.at[k]) for k in range(blocks)]
    for k in range(blocks):
        decays[k].start()
        driving[k].start()

    row_peers = [(row * COLS + lax.rem(col + k, COLS), chan) for k in range(1, COLS)]
    col_peers = [(lax.rem(row + k, rows) * COLS + col, chan) for k in range(1, rows)]
    chan_peers = [(time, lax.rem(chan + k, chans)) for k in range(1, chans)]
    peers = row_peers + col_peers + chan_peers
    barrier = pltpu.get_barrier_semaphore()
    for peer in peers:
        pl.semaphore_signal(barrier, inc=1, device_id=peer, device_id_type=MESH)

    lower[...] = triangle(2 * BLOCK)
    chunks = [slice(k, k + CHUNK) for k in range(0, BLOCK, CHUNK)]

    def cumulate(block):
        decays[block].wait()
        total = jnp.zeros((8, width), F32)
        for here in chunks:
            rate = decay[block, here, :]
            total = total + (rate[:8] + rate[8:])
            rounded[block % 2, here, :] = rate.astype(BF16)
        ends[block : block + 1, :] = jnp.exp2(total.sum(0, keepdims=True) * -log2_scale)
        logs[block] = jnp.dot(lower[:, :BLOCK], rounded[block % 2], preferred_element_type=F32)

    def grow(block):
        driving[block].wait()
        total = jnp.zeros((8, width), F32)
        for here in chunks:
            drive = drives[block, 0, here, :].astype(F32)
            grown = drive * jnp.exp2(logs[block, here, :] * log2_scale)
            total = total + (grown[:8] + grown[8:])
            drives[block, 1, here, :] = (grown - drive).astype(BF16)
        ends[blocks + block : blocks + block + 1, :] = ends[block : block + 1, :] * total.sum(0, keepdims=True)

    def send_row(which):
        for peer in row_peers:
            pltpu.make_async_remote_copy(
                row_buf.at[which, col], row_buf.at[which, col], row_send, row_recv.at[which],
                device_id=peer, device_id_type=MESH,
            ).start()

    def wait_row(which):
        several = row_buf.at[which, pl.ds(0, COLS - 1)]
        pltpu.make_async_copy(several, several, row_recv.at[which]).wait()

    def col_copy(which, k, source):
        return pltpu.make_async_remote_copy(
            col_buf.at[source, which], col_buf.at[source, which], col_send.at[k], col_recv.at[source],
            device_id=col_peers[k], device_id_type=MESH,
        )

    def send_col(which):
        for k in range(rows - 1):
            pl.when(row + k + 1 < rows)(col_copy(which, k, row).start)

    cumulate(0)
    for block in range(blocks):
        if block + 1 < blocks:
            cumulate(block + 1)
        if block + 2 == blocks:
            for b in range(batch):
                first = b * halves
                row_buf[0, col, b : b + 1, :] = functools.reduce(
                    jnp.multiply, [ends[first + k : first + k + 1, :] for k in range(halves)]
                )
            pl.semaphore_wait(barrier, len(peers))
            send_row(0)
        if block >= blocks // 2:
            for k in range(2 * (block - blocks // 2), 2 * (block - blocks // 2) + 2):
                gates[k].start()
        grow(block)

    for b in range(batch):
        first = b * halves
        state = ends[blocks + first : blocks + first + 1, :]
        for k in range(first + 1, first + halves):
            state = ends[k : k + 1, :] * state + ends[blocks + k : blocks + k + 1, :]
        row_buf[1, col, b : b + 1, :] = state
    send_row(1)

    def gate_block(block):
        gates[block].wait()
        local[block] = jnp.dot(lower[...], drives[block].reshape(2 * BLOCK, width), preferred_element_type=F32)
        for here in chunks:
            half = 0.5 * total_length**-0.5
            sigmoid = jnp.tanh(gate[block, here, :].astype(F32) * 0.5) * half + half
            logs[block, here, :] = jnp.exp2(logs[block, here, :] * -log2_scale) * sigmoid

    for block in range(blocks // 2):
        gate_block(block)

    wait_row(0)
    keep_before, keep = jnp.ones((batch, width), F32), jnp.ones((batch, width), F32)
    for j in range(COLS):
        keep = row_buf[0, j] * keep
        keep_before = jnp.where(j < col, keep, keep_before)
    col_buf[row, 0] = keep
    send_col(0)
    gate_block(blocks // 2)

    wait_row(1)
    state = state_before = jnp.zeros((batch, width), F32)
    for j in range(COLS):
        state = row_buf[0, j] * state + row_buf[1, j]
        state_before = jnp.where(j < col, state, state_before)
    col_buf[row, 1] = state
    send_col(1)

    for block in range(blocks // 2 + 1, blocks):
        gate_block(block)

    for k in range(1, rows):
        source = lax.rem(row + k, rows)
        copy = pltpu.make_async_copy(col_buf.at[source], col_buf.at[source], col_recv.at[source])
        pl.when(source < row)(copy.wait)
    entering = jnp.zeros((batch, width), F32)
    for j in range(rows):
        entering = jnp.where(j < row, col_buf[j, 0] * entering + col_buf[j, 1], entering)
    entering = keep_before * entering + state_before

    powers = jnp.zeros((blocks, BLOCK), F32)
    for b in range(batch):
        start = entering[b : b + 1, :]
        for block in range(b * halves, (b + 1) * halves):
            where = block % halves * BLOCK
            squares = []
            for here in chunks:
                gated = logs[block, here, :] * (local[block, here, :] + start)
                gated_ref[b, where + here.start : where + here.stop, :] = gated
                square = gated * gated
                square = sum(square[:, k : k + LANES] for k in range(0, width, LANES))
                squares.append(jnp.concatenate(parts(square), axis=1))
            pick = jnp.where(iota((blocks, 2 * LANES), 0) == block, 1.0, 0.0).astype(BF16)
            powers = powers + lax.dot_general(
                pick, jnp.concatenate(squares, axis=0), NT, preferred_element_type=F32
            )
            if block + 1 < (b + 1) * halves:
                start = ends[block : block + 1, :] * (local[block, BLOCK - 1 :, :] + start)
    power_buf[chan] = powers
    for peer in chan_peers:
        pltpu.make_async_remote_copy(
            power_buf.at[chan], power_buf.at[chan], power_send, power_recv, device_id=peer, device_id_type=MESH
        ).start()
    several = power_buf.at[pl.ds(0, chans - 1)]
    pltpu.make_async_copy(several, several, power_recv).wait()
    power = sum(power_buf[j] for j in range(chans)) / (width * chans)
    scale_ref[...] = lax.rsqrt(power + 1e-06)

    for which in range(2):
        several = row_buf.at[which, pl.ds(0, COLS - 1)]
        pltpu.make_async_copy(several, several, row_send).wait()
    for k in range(rows - 1):
        pl.when(row + k + 1 < rows)(pltpu.make_async_copy(col_buf.at[row], col_buf.at[row], col_send.at[k]).wait)
    several = power_buf.at[pl.ds(0, chans - 1)]
    pltpu.make_async_copy(several, several, power_send).wait()


def scale_kernel(gated_ref, scale_ref, gain_ref, out_hbm, result, factors, sem):
    batch, length, width = result.shape
    blocks = scale_ref.shape[0]
    halves = blocks // batch
    wide = (2 * blocks, blocks * LANES)
    pick = jnp.where(lax.rem(iota(wide, 0), blocks) == iota(wide, 1) // LANES, 1.0, 0.0).astype(BF16)
    factors[...] = lax.dot_general(
        jnp.concatenate(parts(scale_ref[...]), axis=0), pick, TN, preferred_element_type=F32
    )
    gain = gain_ref[...].reshape(1, width)
    for block in range(blocks):
        b, where = block // halves, block % halves * BLOCK
        for k in range(0, BLOCK, CHUNK):
            here = slice(where + k, where + k + CHUNK)
            factor = factors[k : k + CHUNK, block * LANES : (block + 1) * LANES]
            factor = jnp.concatenate([factor] * (width // LANES), axis=1)
            result[b, here, :] = (gated_ref[b, here, :] * factor * gain).astype(result.dtype)
        there = (b, pl.ds(where, BLOCK))
        pltpu.make_async_copy(result.at[there], out_hbm.at[there], sem).start()
    pltpu.make_async_copy(result, out_hbm, sem).wait()


def solution(mesh):
    times, chans = mesh.shape["time"], mesh.shape["chan"]

    def body(decay_rate, drive_in, gate_in, norm_gain):
        batch, length, width = decay_rate.shape
        blocks = batch * length // BLOCK
        rows = times // COLS
        dma = pltpu.SemaphoreType.DMA
        vmem = pl.BlockSpec(memory_space=pltpu.VMEM)
        gated, scale = pl.pallas_call(
            functools.partial(state_kernel, times, chans),
            out_shape=(pltpu.VMEM((batch, length, width), F32), pltpu.VMEM((blocks, BLOCK), F32)),
            in_specs=[pl.BlockSpec(memory_space=pltpu.HBM)] * 3,
            out_specs=(vmem, vmem),
            scratch_shapes=[
                pltpu.VMEM((blocks, BLOCK, width), F32),
                pltpu.VMEM((blocks, 2, BLOCK, width), BF16),
                pltpu.VMEM((blocks, BLOCK, width), BF16),
                pltpu.VMEM((blocks, BLOCK, width), F32),
                pltpu.VMEM((blocks, BLOCK, width), F32),
                pltpu.VMEM((2, BLOCK, width), BF16),
                pltpu.VMEM((BLOCK, 2 * BLOCK), BF16),
                pltpu.VMEM((2 * blocks, width), F32),
                pltpu.VMEM((2, COLS, batch, width), F32),
                pltpu.VMEM((rows, 2, batch, width), F32),
                pltpu.VMEM((chans, blocks, BLOCK), F32),
                dma((blocks,)), dma((blocks,)),
                dma, dma((2,)),
                dma((rows - 1,)), dma((rows,)),
                dma, dma,
            ],
            compiler_params=pltpu.CompilerParams(
                collective_id=0, has_side_effects=True, vmem_limit_bytes=57 * 2**20
            ),
        )(decay_rate, drive_in, gate_in)
        return pl.pallas_call(
            scale_kernel,
            out_shape=jax.ShapeDtypeStruct((batch, length, width), BF16),
            in_specs=[vmem, vmem, vmem],
            out_specs=pl.BlockSpec(memory_space=pltpu.HBM),
            scratch_shapes=[
                pltpu.VMEM((batch, length, width), BF16),
                pltpu.VMEM((BLOCK, blocks * LANES), F32),
                dma,
            ],
            compiler_params=pltpu.CompilerParams(vmem_limit_bytes=16 * 2**20),
        )(gated, scale, norm_gain)

    in_specs = (P(None, "time", "chan"), P(None, "time", "chan"), P(None, "time", "chan"), P("chan"))
    return jax.shard_map(body, mesh=mesh, in_specs=in_specs, out_specs=P(None, "time", "chan"), check_vma=False)
```

time: 37 us -> 26.7 us (0.72)
  Pallas kernels: 32.6 us -> 26.6 us
  local copies, waits for them, and re-layouts: 4.17 us -> 0.01 us
    unnamed x4 -> x2, local copies, waits for them, and re-layouts: 3.48 us -> 0.01 us
    pallas_call x1, Pallas kernels: 27.9 us -> 24.7 us  [body(): pl.pallas_call(functools.partial(state_kernel, times, chans), out_shape=(...]
    pallas_call x1, Pallas kernels: 4.79 us -> 1.89 us  [body(): pl.pallas_call(scale_kernel, out_shape=jax.ShapeDtypeStruct((batch, lengt...]
    reshape x1 -> x0, local copies, waits for them, and re-layouts: 0.69 us -> none  [body(): norm_gain.reshape(1, width)]
where the time goes in v3:
time: 26.7 us; the launch traced here: 26.6 us
  Pallas kernels  26.6 us (100%)
    pallas_call x1, Pallas kernels, body(): pl.pallas_call(functools.partial(state_kernel, times, chans), out_shape=(...  24.7 us
    pallas_call x1, Pallas kernels, body(): pl.pallas_call(scale_kernel, out_shape=jax.ShapeDtypeStruct((batch, lengt...  1.89 us

profile of v3, /device:TPU:32, one launch (start us, length us, event | category | flops | bytes accessed | tf_op | source)
XLA Modules:
  0.0 26.6 jit_solution(18128981247384664728)
XLA Ops:
  0.0 0.0 copy-start
  0.0 24.7 %shard_map.46 = (f32[4,512,640]{2,1,0:T(8,128)S(1)}, f32[8,256]{1,0:T(8,128)S(1)}) custom-call(f32[4,512,640]{2,1,0:T(8,128)} %decay_hbm.1, bf16[4,512,640]{2,1,0:T(8,128)(2,1)} %drive_hbm.1, bf16[4,512,640]{2,1,0:T(8,128)(2,1)} %gate_hbm.1), custom_call_target="tpu_custom_call" | custom-call | tf_op jit(solution)/shard_map/pallas_call | solution.py:245
  24.7 0.0 copy-done
  24.7 1.9 %shard_map.47 = bf16[4,512,640]{2,1,0:T(8,128)(2,1)} custom-call(f32[4,512,640]{2,1,0:T(8,128)S(1)} %get-tuple-element.7.gated_ref, f32[8,256]{1,0:T(8,128)S(1)} %get-tuple-element.8.scale_ref, f32[640]{0:T(1024)S(1)} %copy-done), custom_call_target="tpu_custom_call" | custom-call | tf_op jit(solution)/shard_map/pallas_call | solution.py:271
Async XLA Ops:
  0.0 24.7 %copy-start = (f32[640]{0:T(1024)S(1)}, f32[640]{0:T(1024)}, u32[]{:S(2)}) copy-start(f32[640]{0:T(1024)} %gain_ref.1) | copy-start | bytes 7684

commit v4 on v3

--- a/solution.py
+++ b/solution.py
@@ -67,9 +67,10 @@
 
     lower[...] = triangle(2 * BLOCK)
     chunks = [slice(k, k + CHUNK) for k in range(0, BLOCK, CHUNK)]
+    none = jnp.zeros((1, width), F32)
+    one = jnp.ones((1, width), F32)
 
     def cumulate(block):
-        decays[block].wait()
         total = jnp.zeros((8, width), F32)
         for here in chunks:
             rate = decay[block, here, :]
@@ -79,7 +80,6 @@
         logs[block] = jnp.dot(lower[:, :BLOCK], rounded[block % 2], preferred_element_type=F32)
 
     def grow(block):
-        driving[block].wait()
         total = jnp.zeros((8, width), F32)
         for here in chunks:
             drive = drives[block, 0, here, :].astype(F32)
@@ -88,97 +88,70 @@
             drives[block, 1, here, :] = (grown - drive).astype(BF16)
         ends[blocks + block : blocks + block + 1, :] = ends[block : block + 1, :] * total.sum(0, keepdims=True)
 
-    def send_row(which):
+    def send_row(b):
+        keep, state = one, none
+        for k in range(b * halves, (b + 1) * halves):
+            shrink = ends[k : k + 1, :]
+            keep, state = shrink * keep, shrink * state + ends[blocks + k : blocks + k + 1, :]
+        row_buf[col, b, 0:1, :] = keep
+        row_buf[col, b, 1:2, :] = state
+        if b == 0:
+            pl.semaphore_wait(barrier, len(peers))
         for peer in row_peers:
             pltpu.make_async_remote_copy(
-                row_buf.at[which, col], row_buf.at[which, col], row_send, row_recv.at[which],
+                row_buf.at[col, b], row_buf.at[col, b], row_send, row_recv.at[b],
                 device_id=peer, device_id_type=MESH,
             ).start()
 
-    def wait_row(which):
-        several = row_buf.at[which, pl.ds(0, COLS - 1)]
-        pltpu.make_async_copy(several, several, row_recv.at[which]).wait()
-
-    def col_copy(which, k, source):
-        return pltpu.make_async_remote_copy(
-            col_buf.at[source, which], col_buf.at[source, which], col_send.at[k], col_recv.at[source],
-            device_id=col_peers[k], device_id_type=MESH,
-        )
-
-    def send_col(which):
+    before = {}
+
+    def send_col(b):
+        several = row_buf.at[pl.ds(0, COLS - 1), b]
+        pltpu.make_async_copy(several, several, row_recv.at[b]).wait()
+        keep, state = one, none
+        keep_before, state_before = keep, state
+        for j in range(COLS):
+            keep, state = row_buf[j, b, 0:1, :] * keep, row_buf[j, b, 0:1, :] * state + row_buf[j, b, 1:2, :]
+            keep_before, state_before = jnp.where(j < col, keep, keep_before), jnp.where(j < col, state, state_before)
+        before[b] = keep_before, state_before
+        col_buf[row, b, 0:1, :] = keep
+        col_buf[row, b, 1:2, :] = state
         for k in range(rows - 1):
-            pl.when(row + k + 1 < rows)(col_copy(which, k, row).start)
-
-    cumulate(0)
-    for block in range(blocks):
-        if block + 1 < blocks:
-            cumulate(block + 1)
-        if block + 2 == blocks:
-            for b in range(batch):
-                first = b * halves
-                row_buf[0, col, b : b + 1, :] = functools.reduce(
-                    jnp.multiply, [ends[first + k : first + k + 1, :] for k in range(halves)]
-                )
-            pl.semaphore_wait(barrier, len(peers))
-            send_row(0)
-        if block >= blocks // 2:
-            for k in range(2 * (block - blocks // 2), 2 * (block - blocks // 2) + 2):
-                gates[k].start()
-        grow(block)
-
-    for b in range(batch):
-        first = b * halves
-        state = ends[blocks + first : blocks + first + 1, :]
-        for k in range(first + 1, first + halves):
-            state = ends[k : k + 1, :] * state + ends[blocks + k : blocks + k + 1, :]
-        row_buf[1, col, b : b + 1, :] = state
-    send_row(1)
+            copy = pltpu.make_async_remote_copy(
+                col_buf.at[row, b], col_buf.at[row, b], col_send.at[k], col_recv.at[b, row],
+                device_id=col_peers[k], device_id_type=MESH,
+            )
+            pl.when(row + k + 1 < rows)(copy.start)
+
+    def enter(b):
+        for k in range(1, rows):
+            source = lax.rem(row + k, rows)
+            copy = pltpu.make_async_copy(col_buf.at[source, b], col_buf.at[source, b], col_recv.at[b, source])
+            pl.when(source < row)(copy.wait)
+        state = none
+        for j in range(rows):
+            state = jnp.where(j < row, col_buf[j, b, 0:1, :] * state + col_buf[j, b, 1:2, :], state)
+        keep_before, state_before = before[b]
+        return keep_before * state + state_before
 
     def gate_block(block):
-        gates[block].wait()
         local[block] = jnp.dot(lower[...], drives[block].reshape(2 * BLOCK, width), preferred_element_type=F32)
         for here in chunks:
             half = 0.5 * total_length**-0.5
             sigmoid = jnp.tanh(gate[block, here, :].astype(F32) * 0.5) * half + half
             logs[block, here, :] = jnp.exp2(logs[block, here, :] * -log2_scale) * sigmoid
 
-    for block in range(blocks // 2):
-        gate_block(block)
-
-    wait_row(0)
-    keep_before, keep = jnp.ones((batch, width), F32), jnp.ones((batch, width), F32)
-    for j in range(COLS):
-        keep = row_buf[0, j] * keep
-        keep_before = jnp.where(j < col, keep, keep_before)
-    col_buf[row, 0] = keep
-    send_col(0)
-    gate_block(blocks // 2)
-
-    wait_row(1)
-    state = state_before = jnp.zeros((batch, width), F32)
-    for j in range(COLS):
-        state = row_buf[0, j] * state + row_buf[1, j]
-        state_before = jnp.where(j < col, state, state_before)
-    col_buf[row, 1] = state
-    send_col(1)
-
-    for block in range(blocks // 2 + 1, blocks):
-        gate_block(block)
-
-    for k in range(1, rows):
-        source = lax.rem(row + k, rows)
-        copy = pltpu.make_async_copy(col_buf.at[source], col_buf.at[source], col_recv.at[source])
-        pl.when(source < row)(copy.wait)
-    entering = jnp.zeros((batch, width), F32)
-    for j in range(rows):
-        entering = jnp.where(j < row, col_buf[j, 0] * entering + col_buf[j, 1], entering)
-    entering = keep_before * entering + state_before
-
-    powers = jnp.zeros((blocks, BLOCK), F32)
-    for b in range(batch):
-        start = entering[b : b + 1, :]
+    def gate_batch(b):
         for block in range(b * halves, (b + 1) * halves):
-            where = block % halves * BLOCK
+            gates[block].wait()
+        for block in range(b * halves, (b + 1) * halves):
+            gate_block(block)
+
+    def finish(b):
+        start = enter(b)
+        powers = jnp.zeros((halves, BLOCK), F32)
+        for half in range(halves):
+            block, where = b * halves + half, half * BLOCK
             squares = []
             for here in chunks:
                 gated = logs[block, here, :] * (local[block, here, :] + start)
@@ -186,25 +159,54 @@
                 square = gated * gated
                 square = sum(square[:, k : k + LANES] for k in range(0, width, LANES))
                 squares.append(jnp.concatenate(parts(square), axis=1))
-            pick = jnp.where(iota((blocks, 2 * LANES), 0) == block, 1.0, 0.0).astype(BF16)
+            pick = jnp.where(iota((halves, 2 * LANES), 0) == half, 1.0, 0.0).astype(BF16)
             powers = powers + lax.dot_general(
                 pick, jnp.concatenate(squares, axis=0), NT, preferred_element_type=F32
             )
-            if block + 1 < (b + 1) * halves:
+            if half + 1 < halves:
                 start = ends[block : block + 1, :] * (local[block, BLOCK - 1 :, :] + start)
-    power_buf[chan] = powers
-    for peer in chan_peers:
-        pltpu.make_async_remote_copy(
-            power_buf.at[chan], power_buf.at[chan], power_send, power_recv, device_id=peer, device_id_type=MESH
-        ).start()
+        power_buf[chan, b] = powers
+        for peer in chan_peers:
+            pltpu.make_async_remote_copy(
+                power_buf.at[chan, b], power_buf.at[chan, b], power_send, power_recv,
+                device_id=peer, device_id_type=MESH,
+            ).start()
+
+    decays[0].wait()
+    cumulate(0)
+    for block in range(blocks):
+        if block + 1 < blocks:
+            decays[block + 1].wait()
+        driving[block].wait()
+        if block == blocks // 2:
+            for copy in gates[:blocks // 2]:
+                copy.start()
+        if block + 1 < blocks:
+            cumulate(block + 1)
+        grow(block)
+        if block % halves == halves - 1:
+            send_row(block // halves)
+    for copy in gates[blocks // 2 :]:
+        copy.start()
+
+    gate_batch(0)
+    gate_batch(1)
+    send_col(0)
+    for b in range(2, batch):
+        gate_batch(b)
+        send_col(b - 1)
+    send_col(batch - 1)
+    for b in range(batch):
+        finish(b)
+
     several = power_buf.at[pl.ds(0, chans - 1)]
     pltpu.make_async_copy(several, several, power_recv).wait()
-    power = sum(power_buf[j] for j in range(chans)) / (width * chans)
-    scale_ref[...] = lax.rsqrt(power + 1e-06)
-
-    for which in range(2):
-        several = row_buf.at[which, pl.ds(0, COLS - 1)]
-        pltpu.make_async_copy(several, several, row_send).wait()
+    for b in range(batch):
+        power = sum(power_buf[j, b] for j in range(chans)) / (width * chans)
+        scale_ref[b * halves : (b + 1) * halves, :] = lax.rsqrt(power + 1e-06)
+
+    several = row_buf.at[pl.ds(0, COLS - 1)]
+    pltpu.make_async_copy(several, several, row_send).wait()
     for k in range(rows - 1):
         pl.when(row + k + 1 < rows)(pltpu.make_async_copy(col_buf.at[row], col_buf.at[row], col_send.at[k]).wait)
     several = power_buf.at[pl.ds(0, chans - 1)]
@@ -256,12 +258,12 @@
                 pltpu.VMEM((2, BLOCK, width), BF16),
                 pltpu.VMEM((BLOCK, 2 * BLOCK), BF16),
                 pltpu.VMEM((2 * blocks, width), F32),
-                pltpu.VMEM((2, COLS, batch, width), F32),
-                pltpu.VMEM((rows, 2, batch, width), F32),
-                pltpu.VMEM((chans, blocks, BLOCK), F32),
+                pltpu.VMEM((COLS, batch, 2, width), F32),
+                pltpu.VMEM((rows, batch, 2, width), F32),
+                pltpu.VMEM((chans, batch, length // BLOCK, BLOCK), F32),
                 dma((blocks,)), dma((blocks,)),
-                dma, dma((2,)),
-                dma((rows - 1,)), dma((rows,)),
+                dma, dma((batch,)),
+                dma((rows - 1,)), dma((batch, rows)),
                 dma, dma,
             ],
             compiler_params=pltpu.CompilerParams(

time: 26.7 us -> 25.5 us (0.955)
  Pallas kernels: 26.6 us -> 25.4 us
    pallas_call x1, Pallas kernels: 24.7 us -> 23.5 us  [body(): pl.pallas_call(functools.partial(state_kernel, times, chans), out_shape=(...]
where the time goes in v4:
time: 25.5 us; the launch traced here: 25.4 us
  Pallas kernels  25.4 us (100%)
    pallas_call x1, Pallas kernels, body(): pl.pallas_call(functools.partial(state_kernel, times, chans), out_shape=(...  23.5 us
    pallas_call x1, Pallas kernels, body(): pl.pallas_call(scale_kernel, out_shape=jax.ShapeDtypeStruct((batch, lengt...  1.89 us

profile of v4, /device:TPU:32, one launch (start us, length us, event | category | flops | bytes accessed | tf_op | source)
XLA Modules:
  0.0 25.4 jit_solution(3329751342594249560)
XLA Ops:
  0.0 0.0 copy-start
  0.0 23.5 %shard_map.46 = (f32[4,512,640]{2,1,0:T(8,128)S(1)}, f32[8,256]{1,0:T(8,128)S(1)}) custom-call(f32[4,512,640]{2,1,0:T(8,128)} %decay_hbm.1, bf16[4,512,640]{2,1,0:T(8,128)(2,1)} %drive_hbm.1, bf16[4,512,640]{2,1,0:T(8,128)(2,1)} %gate_hbm.1), custom_call_target="tpu_custom_call" | custom-call | tf_op jit(solution)/shard_map/pallas_call | solution.py:247
  23.5 0.0 copy-done
  23.5 1.9 %shard_map.47 = bf16[4,512,640]{2,1,0:T(8,128)(2,1)} custom-call(f32[4,512,640]{2,1,0:T(8,128)S(1)} %get-tuple-element.7.gated_ref, f32[8,256]{1,0:T(8,128)S(1)} %get-tuple-element.8.scale_ref, f32[640]{0:T(1024)S(1)} %copy-done), custom_call_target="tpu_custom_call" | custom-call | tf_op jit(solution)/shard_map/pallas_call | solution.py:273
Async XLA Ops:
  0.0 23.5 %copy-start = (f32[640]{0:T(1024)S(1)}, f32[640]{0:T(1024)}, u32[]{:S(2)}) copy-start(f32[640]{0:T(1024)} %gain_ref.1) | copy-start | bytes 7684

commit v5 on v4

--- a/solution.py
+++ b/solution.py
@@ -23,9 +23,9 @@
     return lax.broadcasted_iota(jnp.int32, shape, dim)
 
 
-def triangle(width):
+def triangle(width, value):
     row, column = iota((BLOCK, width), 0), iota((BLOCK, width), 1)
-    return jnp.where(lax.rem(column, BLOCK) <= row, 1.0, 0.0).astype(BF16)
+    return jnp.where(lax.rem(column, BLOCK) <= row, value, 0.0).astype(BF16)
 
 
 def parts(x):
@@ -35,7 +35,7 @@
 
 def state_kernel(
     times, chans, decay_hbm, drive_hbm, gate_hbm, gated_ref, scale_ref,
-    decay, drives, gate, logs, local, rounded, lower, ends, row_buf, col_buf, power_buf,
+    decay, drives, gate, logs, local, rounded, fall, lower, ends, row_buf, col_buf, power_buf,
     decay_sem, drive_sem, row_send, row_recv, col_send, col_recv, power_send, power_recv,
 ):
     batch, length, width = decay_hbm.shape
@@ -44,6 +44,7 @@
     rows = times // COLS
     total_length = length * times
     log2_scale = math.log2(math.e) / total_length
+    half = 0.5 * total_length**-0.5
     time, chan = lax.axis_index("time"), lax.axis_index("chan")
     row, col = time // COLS, lax.rem(time, COLS)
 
@@ -53,8 +54,10 @@
     decays = [pltpu.make_async_copy(at(decay_hbm, k), decay.at[k], decay_sem.at[k]) for k in range(blocks)]
     driving = [pltpu.make_async_copy(at(drive_hbm, k), drives.at[k, 0], drive_sem.at[k]) for k in range(blocks)]
     gates = [pltpu.make_async_copy(at(gate_hbm, k), gate.at[k], decay_sem.at[k]) for k in range(blocks)]
+    decays[0].start()
     for k in range(blocks):
-        decays[k].start()
+        if k + 1 < blocks:
+            decays[k + 1].start()
         driving[k].start()
 
     row_peers = [(row * COLS + lax.rem(col + k, COLS), chan) for k in range(1, COLS)]
@@ -65,27 +68,30 @@
     for peer in peers:
         pl.semaphore_signal(barrier, inc=1, device_id=peer, device_id_type=MESH)
 
-    lower[...] = triangle(2 * BLOCK)
+    fall[...] = triangle(BLOCK, -log2_scale)
+    lower[...] = triangle(2 * BLOCK, 1.0)
     chunks = [slice(k, k + CHUNK) for k in range(0, BLOCK, CHUNK)]
     none = jnp.zeros((1, width), F32)
     one = jnp.ones((1, width), F32)
 
-    def cumulate(block):
+    def prepare(block):
         total = jnp.zeros((8, width), F32)
         for here in chunks:
             rate = decay[block, here, :]
             total = total + (rate[:8] + rate[8:])
             rounded[block % 2, here, :] = rate.astype(BF16)
         ends[block : block + 1, :] = jnp.exp2(total.sum(0, keepdims=True) * -log2_scale)
-        logs[block] = jnp.dot(lower[:, :BLOCK], rounded[block % 2], preferred_element_type=F32)
 
     def grow(block):
+        fallen = jnp.dot(fall[...], rounded[block % 2], preferred_element_type=F32)
         total = jnp.zeros((8, width), F32)
         for here in chunks:
+            logs[block, here, :] = fallen[here]
             drive = drives[block, 0, here, :].astype(F32)
-            grown = drive * jnp.exp2(logs[block, here, :] * log2_scale)
-            total = total + (grown[:8] + grown[8:])
-            drives[block, 1, here, :] = (grown - drive).astype(BF16)
+            added = drive * (jnp.exp2(-fallen[here]) - 1.0)
+            drives[block, 1, here, :] = added.astype(BF16)
+            added = added + drive
+            total = total + (added[:8] + added[8:])
         ends[blocks + block : blocks + block + 1, :] = ends[block : block + 1, :] * total.sum(0, keepdims=True)
 
     def send_row(b):
@@ -95,8 +101,8 @@
             keep, state = shrink * keep, shrink * state + ends[blocks + k : blocks + k + 1, :]
         row_buf[col, b, 0:1, :] = keep
         row_buf[col, b, 1:2, :] = state
-        if b == 0:
-            pl.semaphore_wait(barrier, len(peers))
+
+    def start_row(b):
         for peer in row_peers:
             pltpu.make_async_remote_copy(
                 row_buf.at[col, b], row_buf.at[col, b], row_send, row_recv.at[b],
@@ -118,16 +124,15 @@
         col_buf[row, b, 1:2, :] = state
         for k in range(rows - 1):
             copy = pltpu.make_async_remote_copy(
-                col_buf.at[row, b], col_buf.at[row, b], col_send.at[k], col_recv.at[b, row],
+                col_buf.at[row, b], col_buf.at[row, b], col_send, col_recv.at[b],
                 device_id=col_peers[k], device_id_type=MESH,
             )
             pl.when(row + k + 1 < rows)(copy.start)
 
     def enter(b):
         for k in range(1, rows):
-            source = lax.rem(row + k, rows)
-            copy = pltpu.make_async_copy(col_buf.at[source, b], col_buf.at[source, b], col_recv.at[b, source])
-            pl.when(source < row)(copy.wait)
+            several = col_buf.at[pl.ds(0, k), b]
+            pl.when(row == k)(pltpu.make_async_copy(several, several, col_recv.at[b]).wait)
         state = none
         for j in range(rows):
             state = jnp.where(j < row, col_buf[j, b, 0:1, :] * state + col_buf[j, b, 1:2, :], state)
@@ -137,9 +142,8 @@
     def gate_block(block):
         local[block] = jnp.dot(lower[...], drives[block].reshape(2 * BLOCK, width), preferred_element_type=F32)
         for here in chunks:
-            half = 0.5 * total_length**-0.5
-            sigmoid = jnp.tanh(gate[block, here, :].astype(F32) * 0.5) * half + half
-            logs[block, here, :] = jnp.exp2(logs[block, here, :] * -log2_scale) * sigmoid
+            opening = jnp.tanh((gate[block, here, :] * 0.5).astype(F32)) + 1.0
+            logs[block, here, :] = jnp.exp2(logs[block, here, :]) * opening
 
     def gate_batch(b):
         for block in range(b * halves, (b + 1) * halves):
@@ -150,8 +154,8 @@
     def finish(b):
         start = enter(b)
         powers = jnp.zeros((halves, BLOCK), F32)
-        for half in range(halves):
-            block, where = b * halves + half, half * BLOCK
+        for part in range(halves):
+            block, where = b * halves + part, part * BLOCK
             squares = []
             for here in chunks:
                 gated = logs[block, here, :] * (local[block, here, :] + start)
@@ -159,11 +163,11 @@
                 square = gated * gated
                 square = sum(square[:, k : k + LANES] for k in range(0, width, LANES))
                 squares.append(jnp.concatenate(parts(square), axis=1))
-            pick = jnp.where(iota((halves, 2 * LANES), 0) == half, 1.0, 0.0).astype(BF16)
+            pick = jnp.where(iota((halves, 2 * LANES), 0) == part, 1.0, 0.0).astype(BF16)
             powers = powers + lax.dot_general(
                 pick, jnp.concatenate(squares, axis=0), NT, preferred_element_type=F32
             )
-            if half + 1 < halves:
+            if part + 1 < halves:
                 start = ends[block : block + 1, :] * (local[block, BLOCK - 1 :, :] + start)
         power_buf[chan, b] = powers
         for peer in chan_peers:
@@ -173,7 +177,7 @@
             ).start()
 
     decays[0].wait()
-    cumulate(0)
+    prepare(0)
     for block in range(blocks):
         if block + 1 < blocks:
             decays[block + 1].wait()
@@ -181,11 +185,17 @@
         if block == blocks // 2:
             for copy in gates[:blocks // 2]:
                 copy.start()
+        grow(block)
         if block + 1 < blocks:
-            cumulate(block + 1)
-        grow(block)
-        if block % halves == halves - 1:
+            prepare(block + 1)
+        if block % halves == halves - 1 and block + 1 < blocks:
             send_row(block // halves)
+            if block + 1 + halves == blocks:
+                pl.semaphore_wait(barrier, len(peers))
+                for b in range(batch - 1):
+                    start_row(b)
+    send_row(batch - 1)
+    start_row(batch - 1)
     for copy in gates[blocks // 2 :]:
         copy.start()
 
@@ -202,13 +212,14 @@
     several = power_buf.at[pl.ds(0, chans - 1)]
     pltpu.make_async_copy(several, several, power_recv).wait()
     for b in range(batch):
-        power = sum(power_buf[j, b] for j in range(chans)) / (width * chans)
-        scale_ref[b * halves : (b + 1) * halves, :] = lax.rsqrt(power + 1e-06)
+        power = sum(power_buf[j, b] for j in range(chans)) * (half * half / (width * chans))
+        scale_ref[b * halves : (b + 1) * halves, :] = half * lax.rsqrt(power + 1e-06)
 
     several = row_buf.at[pl.ds(0, COLS - 1)]
     pltpu.make_async_copy(several, several, row_send).wait()
-    for k in range(rows - 1):
-        pl.when(row + k + 1 < rows)(pltpu.make_async_copy(col_buf.at[row], col_buf.at[row], col_send.at[k]).wait)
+    for k in range(1, rows):
+        several = col_buf.at[pl.ds(0, k)]
+        pl.when(row + k + 1 == rows)(pltpu.make_async_copy(several, several, col_send).wait)
     several = power_buf.at[pl.ds(0, chans - 1)]
     pltpu.make_async_copy(several, several, power_send).wait()
 
@@ -256,6 +267,7 @@
                 pltpu.VMEM((blocks, BLOCK, width), F32),
                 pltpu.VMEM((blocks, BLOCK, width), F32),
                 pltpu.VMEM((2, BLOCK, width), BF16),
+                pltpu.VMEM((BLOCK, BLOCK), BF16),
                 pltpu.VMEM((BLOCK, 2 * BLOCK), BF16),
                 pltpu.VMEM((2 * blocks, width), F32),
                 pltpu.VMEM((COLS, batch, 2, width), F32),
@@ -263,7 +275,7 @@
                 pltpu.VMEM((chans, batch, length // BLOCK, BLOCK), F32),
                 dma((blocks,)), dma((blocks,)),
                 dma, dma((batch,)),
-                dma((rows - 1,)), dma((batch, rows)),
+                dma, dma((batch,)),
                 dma, dma,
             ],
             compiler_params=pltpu.CompilerParams(

time: 25.5 us -> 26.1 us (1.024)
  Pallas kernels: 25.4 us -> 26 us
    pallas_call x1, Pallas kernels: 23.5 us -> 24.1 us  [body(): pl.pallas_call(functools.partial(state_kernel, times, chans), out_shape=(...]
where the time goes in v5:
time: 26.1 us; the launch traced here: 26 us
  Pallas kernels  26 us (100%)
    pallas_call x1, Pallas kernels, body(): pl.pallas_call(functools.partial(state_kernel, times, chans), out_shape=(...  24.1 us
    pallas_call x1, Pallas kernels, body(): pl.pallas_call(scale_kernel, out_shape=jax.ShapeDtypeStruct((batch, lengt...  1.89 us

profile of v5, /device:TPU:32, one launch (start us, length us, event | category | flops | bytes accessed | tf_op | source)
XLA Modules:
  0.0 26.0 jit_solution(6754783446061040587)
XLA Ops:
  0.0 0.0 copy-start
  0.0 24.1 %shard_map.46 = (f32[4,512,640]{2,1,0:T(8,128)S(1)}, f32[8,256]{1,0:T(8,128)S(1)}) custom-call(f32[4,512,640]{2,1,0:T(8,128)} %decay_hbm.1, bf16[4,512,640]{2,1,0:T(8,128)(2,1)} %drive_hbm.1, bf16[4,512,640]{2,1,0:T(8,128)(2,1)} %gate_hbm.1), custom_call_target="tpu_custom_call" | custom-call | tf_op jit(solution)/shard_map/pallas_call | solution.py:258
  24.1 0.0 copy-done
  24.1 1.9 %shard_map.47 = bf16[4,512,640]{2,1,0:T(8,128)(2,1)} custom-call(f32[4,512,640]{2,1,0:T(8,128)S(1)} %get-tuple-element.7.gated_ref, f32[8,256]{1,0:T(8,128)S(1)} %get-tuple-element.8.scale_ref, f32[640]{0:T(1024)S(1)} %copy-done), custom_call_target="tpu_custom_call" | custom-call | tf_op jit(solution)/shard_map/pallas_call | solution.py:285
Async XLA Ops:
  0.0 24.1 %copy-start = (f32[640]{0:T(1024)S(1)}, f32[640]{0:T(1024)}, u32[]{:S(2)}) copy-start(f32[640]{0:T(1024)} %gain_ref.1) | copy-start | bytes 7684

commit v6 on v5

--- a/solution.py
+++ b/solution.py
@@ -199,13 +199,10 @@
     for copy in gates[blocks // 2 :]:
         copy.start()
 
-    gate_batch(0)
-    gate_batch(1)
-    send_col(0)
-    for b in range(2, batch):
+    for b in range(batch):
         gate_batch(b)
-        send_col(b - 1)
-    send_col(batch - 1)
+    for b in range(batch):
+        send_col(b)
     for b in range(batch):
         finish(b)
 

time: 26.1 us -> 25.5 us (0.977)
  Pallas kernels: 26 us -> 25.4 us
    pallas_call x1, Pallas kernels: 24.1 us -> 23.5 us  [body(): pl.pallas_call(functools.partial(state_kernel, times, chans), out_shape=(...]
where the time goes in v6:
time: 25.5 us
  Pallas kernels  25.4 us (100%)
    pallas_call x1, Pallas kernels, body(): pl.pallas_call(functools.partial(state_kernel, times, chans), out_shape=(...  23.5 us
    pallas_call x1, Pallas kernels, body(): pl.pallas_call(scale_kernel, out_shape=jax.ShapeDtypeStruct((batch, lengt...  1.89 us

profile of v6, /device:TPU:32, one launch (start us, length us, event | category | flops | bytes accessed | tf_op | source)
XLA Modules:
  0.0 25.5 jit_solution(12958739344828502142)
XLA Ops:
  0.0 0.0 copy-start
  0.0 23.5 %shard_map.46 = (f32[4,512,640]{2,1,0:T(8,128)S(1)}, f32[8,256]{1,0:T(8,128)S(1)}) custom-call(f32[4,512,640]{2,1,0:T(8,128)} %decay_hbm.1, bf16[4,512,640]{2,1,0:T(8,128)(2,1)} %drive_hbm.1, bf16[4,512,640]{2,1,0:T(8,128)(2,1)} %gate_hbm.1), custom_call_target="tpu_custom_call" | custom-call | tf_op jit(solution)/shard_map/pallas_call | solution.py:255
  23.6 0.0 copy-done
  23.6 1.9 %shard_map.47 = bf16[4,512,640]{2,1,0:T(8,128)(2,1)} custom-call(f32[4,512,640]{2,1,0:T(8,128)S(1)} %get-tuple-element.7.gated_ref, f32[8,256]{1,0:T(8,128)S(1)} %get-tuple-element.8.scale_ref, f32[640]{0:T(1024)S(1)} %copy-done), custom_call_target="tpu_custom_call" | custom-call | tf_op jit(solution)/shard_map/pallas_call | solution.py:282
Async XLA Ops:
  0.0 23.6 %copy-start = (f32[640]{0:T(1024)S(1)}, f32[640]{0:T(1024)}, u32[]{:S(2)}) copy-start(f32[640]{0:T(1024)} %gain_ref.1) | copy-start | bytes 7684

commit v7 on v6

--- a/solution.py
+++ b/solution.py
@@ -68,7 +68,7 @@
     for peer in peers:
         pl.semaphore_signal(barrier, inc=1, device_id=peer, device_id_type=MESH)
 
-    fall[...] = triangle(BLOCK, -log2_scale)
+    fall[...] = triangle(BLOCK, log2_scale)
     lower[...] = triangle(2 * BLOCK, 1.0)
     chunks = [slice(k, k + CHUNK) for k in range(0, BLOCK, CHUNK)]
     none = jnp.zeros((1, width), F32)
@@ -82,16 +82,18 @@
             rounded[block % 2, here, :] = rate.astype(BF16)
         ends[block : block + 1, :] = jnp.exp2(total.sum(0, keepdims=True) * -log2_scale)
 
-    def grow(block):
-        fallen = jnp.dot(fall[...], rounded[block % 2], preferred_element_type=F32)
+    def mixed(block):
         total = jnp.zeros((8, width), F32)
-        for here in chunks:
-            logs[block, here, :] = fallen[here]
-            drive = drives[block, 0, here, :].astype(F32)
-            added = drive * (jnp.exp2(-fallen[here]) - 1.0)
-            drives[block, 1, here, :] = added.astype(BF16)
-            added = added + drive
-            total = total + (added[:8] + added[8:])
+        pieces = [(0, 256, chunks[:3]), (256, 512, chunks[3:6]), (512, width, chunks[6:])]
+        for left, right, some in pieces:
+            if block + 1 < blocks:
+                logs[block + 1, :, left:right] = jnp.dot(
+                    fall[...], rounded[(block + 1) % 2, :, left:right], preferred_element_type=F32
+                )
+            for here in some:
+                drive, growth = drives[block, 0, here, :], jnp.exp2(logs[block, here, :])
+                grown = drive.astype(F32) * growth
+                total = total + (grown[:8] + grown[8:])
         ends[blocks + block : blocks + block + 1, :] = ends[block : block + 1, :] * total.sum(0, keepdims=True)
 
     def send_row(b):
@@ -129,10 +131,12 @@
             )
             pl.when(row + k + 1 < rows)(copy.start)
 
-    def enter(b):
+    def wait_col(b):
         for k in range(1, rows):
             several = col_buf.at[pl.ds(0, k), b]
             pl.when(row == k)(pltpu.make_async_copy(several, several, col_recv.at[b]).wait)
+
+    def enter(b):
         state = none
         for j in range(rows):
             state = jnp.where(j < row, col_buf[j, b, 0:1, :] * state + col_buf[j, b, 1:2, :], state)
@@ -143,13 +147,21 @@
         local[block] = jnp.dot(lower[...], drives[block].reshape(2 * BLOCK, width), preferred_element_type=F32)
         for here in chunks:
             opening = jnp.tanh((gate[block, here, :] * 0.5).astype(F32)) + 1.0
-            logs[block, here, :] = jnp.exp2(logs[block, here, :]) * opening
+            logs[block, here, :] = jnp.exp2(-logs[block, here, :]) * opening
+
+    def spread(b):
+        for block in range(b * halves, (b + 1) * halves):
+            for here in chunks:
+                growth = jnp.exp2(logs[block, here, :]) - 1.0
+                drives[block, 1, here, :] = growth.astype(BF16) * drives[block, 0, here, :]
 
     def gate_batch(b):
         for block in range(b * halves, (b + 1) * halves):
             gates[block].wait()
         for block in range(b * halves, (b + 1) * halves):
             gate_block(block)
+        if b + 1 < batch:
+            spread(b + 1)
 
     def finish(b):
         start = enter(b)
@@ -170,6 +182,8 @@
             if part + 1 < halves:
                 start = ends[block : block + 1, :] * (local[block, BLOCK - 1 :, :] + start)
         power_buf[chan, b] = powers
+
+    def send_power(b):
         for peer in chan_peers:
             pltpu.make_async_remote_copy(
                 power_buf.at[chan, b], power_buf.at[chan, b], power_send, power_recv,
@@ -178,39 +192,44 @@
 
     decays[0].wait()
     prepare(0)
+    decays[1].wait()
+    logs[0] = jnp.dot(fall[...], rounded[0], preferred_element_type=F32)
+    prepare(1)
     for block in range(blocks):
-        if block + 1 < blocks:
-            decays[block + 1].wait()
+        if block + 2 < blocks:
+            decays[block + 2].wait()
         driving[block].wait()
         if block == blocks // 2:
             for copy in gates[:blocks // 2]:
                 copy.start()
-        grow(block)
-        if block + 1 < blocks:
-            prepare(block + 1)
+        mixed(block)
+        if block + 2 < blocks:
+            prepare(block + 2)
         if block % halves == halves - 1 and block + 1 < blocks:
-            send_row(block // halves)
-            if block + 1 + halves == blocks:
+            b = block // halves
+            send_row(b)
+            if b == 1:
                 pl.semaphore_wait(barrier, len(peers))
-                for b in range(batch - 1):
-                    start_row(b)
+                start_row(0)
+            if b >= 1:
+                start_row(b)
     send_row(batch - 1)
     start_row(batch - 1)
     for copy in gates[blocks // 2 :]:
         copy.start()
 
+    spread(0)
     for b in range(batch):
         gate_batch(b)
     for b in range(batch):
         send_col(b)
-    for b in range(batch):
-        finish(b)
-
-    several = power_buf.at[pl.ds(0, chans - 1)]
-    pltpu.make_async_copy(several, several, power_recv).wait()
-    for b in range(batch):
-        power = sum(power_buf[j, b] for j in range(chans)) * (half * half / (width * chans))
-        scale_ref[b * halves : (b + 1) * halves, :] = half * lax.rsqrt(power + 1e-06)
+    for group in (range(2), range(2, batch)):
+        for b in group:
+            wait_col(b)
+        for b in group:
+            finish(b)
+        for b in group:
+            send_power(b)
 
     several = row_buf.at[pl.ds(0, COLS - 1)]
     pltpu.make_async_copy(several, several, row_send).wait()
@@ -219,6 +238,10 @@
         pl.when(row + k + 1 == rows)(pltpu.make_async_copy(several, several, col_send).wait)
     several = power_buf.at[pl.ds(0, chans - 1)]
     pltpu.make_async_copy(several, several, power_send).wait()
+    pltpu.make_async_copy(several, several, power_recv).wait()
+    for b in range(batch):
+        power = sum(power_buf[j, b] for j in range(chans)) * (half * half / (width * chans))
+        scale_ref[b * halves : (b + 1) * halves, :] = half * lax.rsqrt(power + 1e-06)
 
 
 def scale_kernel(gated_ref, scale_ref, gain_ref, out_hbm, result, factors, sem):
@@ -230,16 +253,21 @@
     factors[...] = lax.dot_general(
         jnp.concatenate(parts(scale_ref[...]), axis=0), pick, TN, preferred_element_type=F32
     )
-    gain = gain_ref[...].reshape(1, width)
-    for block in range(blocks):
-        b, where = block // halves, block % halves * BLOCK
+    gain = jnp.broadcast_to(gain_ref[...].reshape(1, width), (8, width))
+
+    def write(block, carry):
+        b, where = block // halves, lax.rem(block, halves) * BLOCK
+        lane = pl.ds(pl.multiple_of(block * LANES, LANES), LANES)
         for k in range(0, BLOCK, CHUNK):
-            here = slice(where + k, where + k + CHUNK)
-            factor = factors[k : k + CHUNK, block * LANES : (block + 1) * LANES]
-            factor = jnp.concatenate([factor] * (width // LANES), axis=1)
-            result[b, here, :] = (gated_ref[b, here, :] * factor * gain).astype(result.dtype)
-        there = (b, pl.ds(where, BLOCK))
+            here = pl.ds(pl.multiple_of(where + k, CHUNK), CHUNK)
+            factor = jnp.concatenate([factors[k : k + CHUNK, lane]] * (width // LANES), axis=1)
+            factor = factor * jnp.concatenate([gain] * (CHUNK // 8), axis=0)
+            result[b, here, :] = (gated_ref[b, here, :] * factor).astype(result.dtype)
+        there = (b, pl.ds(pl.multiple_of(where, BLOCK), BLOCK))
         pltpu.make_async_copy(result.at[there], out_hbm.at[there], sem).start()
+        return carry
+
+    lax.fori_loop(0, blocks, write, 0)
     pltpu.make_async_copy(result, out_hbm, sem).wait()
 
 

time: 25.5 us -> 25.2 us (0.988)
  Pallas kernels: 25.4 us -> 25.1 us
    pallas_call x1, Pallas kernels: 23.5 us -> 23.3 us  [body(): pl.pallas_call(functools.partial(state_kernel, times, chans), out_shape=(...]
where the time goes in v7:
time: 25.2 us
  Pallas kernels  25.1 us (100%)
    pallas_call x1, Pallas kernels, body(): pl.pallas_call(functools.partial(state_kernel, times, chans), out_shape=(...  23.3 us
    pallas_call x1, Pallas kernels, body(): pl.pallas_call(scale_kernel, out_shape=jax.ShapeDtypeStruct((batch, lengt...  1.89 us

profile of v7, /device:TPU:32, one launch (start us, length us, event | category | flops | bytes accessed | tf_op | source)
XLA Modules:
  0.0 25.2 jit_solution(6896232318607117448)
XLA Ops:
  0.0 0.0 copy-start
  0.0 23.3 %shard_map.46 = (f32[4,512,640]{2,1,0:T(8,128)S(1)}, f32[8,256]{1,0:T(8,128)S(1)}) custom-call(f32[4,512,640]{2,1,0:T(8,128)} %decay_hbm.1, bf16[4,512,640]{2,1,0:T(8,128)(2,1)} %drive_hbm.1, bf16[4,512,640]{2,1,0:T(8,128)(2,1)} %gate_hbm.1), custom_call_target="tpu_custom_call" | custom-call | tf_op jit(solution)/shard_map/pallas_call | solution.py:283
  23.3 0.0 copy-done
  23.3 1.9 %shard_map.47 = bf16[4,512,640]{2,1,0:T(8,128)(2,1)} custom-call(f32[4,512,640]{2,1,0:T(8,128)S(1)} %get-tuple-element.7.gated_ref, f32[8,256]{1,0:T(8,128)S(1)} %get-tuple-element.8.scale_ref, f32[640]{0:T(1024)S(1)} %copy-done), custom_call_target="tpu_custom_call" | custom-call | tf_op jit(solution)/shard_map/pallas_call | solution.py:310
Async XLA Ops:
  0.0 23.3 %copy-start = (f32[640]{0:T(1024)S(1)}, f32[640]{0:T(1024)}, u32[]{:S(2)}) copy-start(f32[640]{0:T(1024)} %gain_ref.1) | copy-start | bytes 7684

commit v8 on v7

--- a/solution.py
+++ b/solution.py
@@ -13,6 +13,7 @@
 LANES = 128
 CHUNK = 16
 COLS = 8
+CORES = 2
 F32 = jnp.float32
 BF16 = jnp.bfloat16
 NT = (((1,), (1,)), ((), ()))
@@ -34,9 +35,9 @@
 
 
 def state_kernel(
-    times, chans, decay_hbm, drive_hbm, gate_hbm, gated_ref, scale_ref,
-    decay, drives, gate, logs, local, rounded, fall, lower, ends, row_buf, col_buf, power_buf,
-    decay_sem, drive_sem, row_send, row_recv, col_send, col_recv, power_send, power_recv,
+    times, chans, decay_hbm, drive_hbm, gate_hbm, gain_hbm, gated_ref, scale_ref,
+    decay, drives, gate, gain, logs, local, rounded, fall, lower, ends, row_buf, col_buf, power_buf,
+    load_sem, row_send, row_recv, col_send, col_recv, power_send, power_recv,
 ):
     batch, length, width = decay_hbm.shape
     halves = length // BLOCK
@@ -51,17 +52,34 @@
     def at(ref, block):
         return ref.at[block // halves, pl.ds(block % halves * BLOCK, BLOCK), :]
 
-    decays = [pltpu.make_async_copy(at(decay_hbm, k), decay.at[k], decay_sem.at[k]) for k in range(blocks)]
-    driving = [pltpu.make_async_copy(at(drive_hbm, k), drives.at[k, 0], drive_sem.at[k]) for k in range(blocks)]
-    gates = [pltpu.make_async_copy(at(gate_hbm, k), gate.at[k], decay_sem.at[k]) for k in range(blocks)]
+    def load(source, target, slot):
+        return pltpu.make_async_copy(source, target, load_sem.at[slot])
+
+    def wait_pair(slot, halves_of_pair):
+        several = drives.at[pl.ds(0, halves_of_pair), 0]
+        pltpu.make_async_copy(several, several, load_sem.at[slot]).wait()
+
+    decays = [load(at(decay_hbm, k), decay.at[k], k) for k in range(blocks)]
+    driving = [load(at(drive_hbm, k), drives.at[k, 0], k + 2) for k in range(blocks)]
+    gates = [load(at(gate_hbm, k), gate.at[k], k // halves) for k in range(blocks)]
+    gains = load(gain_hbm, gain, blocks + 2)
     decays[0].start()
+    decays[1].start()
     for k in range(blocks):
-        if k + 1 < blocks:
-            decays[k + 1].start()
         driving[k].start()
-
-    row_peers = [(row * COLS + lax.rem(col + k, COLS), chan) for k in range(1, COLS)]
-    col_peers = [(lax.rem(row + k, rows) * COLS + col, chan) for k in range(1, rows)]
+        if k + 2 < blocks:
+            decays[k + 2].start()
+
+    chips = COLS // CORES
+    chip, core = col // CORES, lax.rem(col, CORES)
+    leads = core == CORES - 1
+    row_peers = [
+        (row * COLS + lax.rem(chip + k, chips) * CORES + c, chan) for c in reversed(range(CORES)) for k in range(1, chips)
+    ]
+    row_peers += [(row * COLS + chip * CORES + lax.rem(core + k, CORES), chan) for k in range(1, CORES)]
+    col_peers = [
+        (lax.rem(row + k, rows) * COLS + chip * CORES + c, chan) for k in range(1, rows) for c in range(CORES)
+    ]
     chan_peers = [(time, lax.rem(chan + k, chans)) for k in range(1, chans)]
     peers = row_peers + col_peers + chan_peers
     barrier = pltpu.get_barrier_semaphore()
@@ -124,12 +142,12 @@
         before[b] = keep_before, state_before
         col_buf[row, b, 0:1, :] = keep
         col_buf[row, b, 1:2, :] = state
-        for k in range(rows - 1):
+        for i, peer in enumerate(col_peers):
             copy = pltpu.make_async_remote_copy(
-                col_buf.at[row, b], col_buf.at[row, b], col_send, col_recv.at[b],
-                device_id=col_peers[k], device_id_type=MESH,
+                col_buf.at[row, b], col_buf.at[row, b], col_send.at[i % CORES], col_recv.at[b],
+                device_id=peer, device_id_type=MESH,
             )
-            pl.when(row + k + 1 < rows)(copy.start)
+            pl.when(jnp.logical_and(leads, row + i // CORES + 1 < rows))(copy.start)
 
     def wait_col(b):
         for k in range(1, rows):
@@ -156,8 +174,7 @@
                 drives[block, 1, here, :] = growth.astype(BF16) * drives[block, 0, here, :]
 
     def gate_batch(b):
-        for block in range(b * halves, (b + 1) * halves):
-            gates[block].wait()
+        wait_pair(b, halves)
         for block in range(b * halves, (b + 1) * halves):
             gate_block(block)
         if b + 1 < batch:
@@ -192,15 +209,13 @@
 
     decays[0].wait()
     prepare(0)
+    logs[0] = jnp.dot(fall[...], rounded[0], preferred_element_type=F32)
     decays[1].wait()
-    logs[0] = jnp.dot(fall[...], rounded[0], preferred_element_type=F32)
     prepare(1)
     for block in range(blocks):
-        if block + 2 < blocks:
-            decays[block + 2].wait()
-        driving[block].wait()
+        wait_pair(block + 2, 3 if block + 2 < blocks else 1)
         if block == blocks // 2:
-            for copy in gates[:blocks // 2]:
+            for copy in gates[: blocks // 2]:
                 copy.start()
         mixed(block)
         if block + 2 < blocks:
@@ -217,13 +232,14 @@
     start_row(batch - 1)
     for copy in gates[blocks // 2 :]:
         copy.start()
+    gains.start()
 
     spread(0)
     for b in range(batch):
         gate_batch(b)
     for b in range(batch):
         send_col(b)
-    for group in (range(2), range(2, batch)):
+    for group in (range(2), *([b] for b in range(2, batch))):
         for b in group:
             wait_col(b)
         for b in group:
@@ -231,11 +247,24 @@
         for b in group:
             send_power(b)
 
+    gains.wait()
+    by_gain = jnp.broadcast_to(gain[...].reshape(1, width), (CHUNK, width))
+
+    def weigh(i, carry):
+        here = pl.ds(pl.multiple_of(i * CHUNK, CHUNK), CHUNK)
+        for b in range(batch):
+            gated_ref[b, here, :] = gated_ref[b, here, :] * by_gain
+        return carry
+
+    lax.fori_loop(0, length // CHUNK, weigh, 0)
+
     several = row_buf.at[pl.ds(0, COLS - 1)]
     pltpu.make_async_copy(several, several, row_send).wait()
     for k in range(1, rows):
         several = col_buf.at[pl.ds(0, k)]
-        pl.when(row + k + 1 == rows)(pltpu.make_async_copy(several, several, col_send).wait)
+        for c in range(CORES):
+            copy = pltpu.make_async_copy(several, several, col_send.at[c])
+            pl.when(jnp.logical_and(leads, row + k + 1 == rows))(copy.wait)
     several = power_buf.at[pl.ds(0, chans - 1)]
     pltpu.make_async_copy(several, several, power_send).wait()
     pltpu.make_async_copy(several, several, power_recv).wait()
@@ -244,7 +273,7 @@
         scale_ref[b * halves : (b + 1) * halves, :] = half * lax.rsqrt(power + 1e-06)
 
 
-def scale_kernel(gated_ref, scale_ref, gain_ref, out_hbm, result, factors, sem):
+def scale_kernel(gated_ref, scale_ref, out_hbm, result, factors, sem):
     batch, length, width = result.shape
     blocks = scale_ref.shape[0]
     halves = blocks // batch
@@ -253,7 +282,6 @@
     factors[...] = lax.dot_general(
         jnp.concatenate(parts(scale_ref[...]), axis=0), pick, TN, preferred_element_type=F32
     )
-    gain = jnp.broadcast_to(gain_ref[...].reshape(1, width), (8, width))
 
     def write(block, carry):
         b, where = block // halves, lax.rem(block, halves) * BLOCK
@@ -261,7 +289,6 @@
         for k in range(0, BLOCK, CHUNK):
             here = pl.ds(pl.multiple_of(where + k, CHUNK), CHUNK)
             factor = jnp.concatenate([factors[k : k + CHUNK, lane]] * (width // LANES), axis=1)
-            factor = factor * jnp.concatenate([gain] * (CHUNK // 8), axis=0)
             result[b, here, :] = (gated_ref[b, here, :] * factor).astype(result.dtype)
         there = (b, pl.ds(pl.multiple_of(where, BLOCK), BLOCK))
         pltpu.make_async_copy(result.at[there], out_hbm.at[there], sem).start()
@@ -283,12 +310,13 @@
         gated, scale = pl.pallas_call(
             functools.partial(state_kernel, times, chans),
             out_shape=(pltpu.VMEM((batch, length, width), F32), pltpu.VMEM((blocks, BLOCK), F32)),
-            in_specs=[pl.BlockSpec(memory_space=pltpu.HBM)] * 3,
+            in_specs=[pl.BlockSpec(memory_space=pltpu.HBM)] * 4,
             out_specs=(vmem, vmem),
             scratch_shapes=[
                 pltpu.VMEM((blocks, BLOCK, width), F32),
                 pltpu.VMEM((blocks, 2, BLOCK, width), BF16),
                 pltpu.VMEM((blocks, BLOCK, width), BF16),
+                pltpu.VMEM((width,), F32),
                 pltpu.VMEM((blocks, BLOCK, width), F32),
                 pltpu.VMEM((blocks, BLOCK, width), F32),
                 pltpu.VMEM((2, BLOCK, width), BF16),
@@ -298,19 +326,19 @@
                 pltpu.VMEM((COLS, batch, 2, width), F32),
                 pltpu.VMEM((rows, batch, 2, width), F32),
                 pltpu.VMEM((chans, batch, length // BLOCK, BLOCK), F32),
-                dma((blocks,)), dma((blocks,)),
+                dma((blocks + 3,)),
                 dma, dma((batch,)),
-                dma, dma((batch,)),
+                dma((CORES,)), dma((batch,)),
                 dma, dma,
             ],
             compiler_params=pltpu.CompilerParams(
                 collective_id=0, has_side_effects=True, vmem_limit_bytes=57 * 2**20
             ),
-        )(decay_rate, drive_in, gate_in)
+        )(decay_rate, drive_in, gate_in, norm_gain)
         return pl.pallas_call(
             scale_kernel,
             out_shape=jax.ShapeDtypeStruct((batch, length, width), BF16),
-            in_specs=[vmem, vmem, vmem],
+            in_specs=[vmem, vmem],
             out_specs=pl.BlockSpec(memory_space=pltpu.HBM),
             scratch_shapes=[
                 pltpu.VMEM((batch, length, width), BF16),
@@ -318,7 +346,7 @@
                 dma,
             ],
             compiler_params=pltpu.CompilerParams(vmem_limit_bytes=16 * 2**20),
-        )(gated, scale, norm_gain)
+        )(gated, scale)
 
     in_specs = (P(None, "time", "chan"), P(None, "time", "chan"), P(None, "time", "chan"), P("chan"))
     return jax.shard_map(body, mesh=mesh, in_specs=in_specs, out_specs=P(None, "time", "chan"), check_vma=False)

time: 25.2 us -> 24 us (0.952)
  Pallas kernels: 25.1 us -> 23.9 us
    pallas_call x1, Pallas kernels: 23.3 us -> 22 us  [body(): pl.pallas_call(functools.partial(state_kernel, times, chans), out_shape=(...]
where the time goes in v8:
time: 24 us; the launch traced here: 23.9 us
  Pallas kernels  23.9 us (100%)
    pallas_call x1, Pallas kernels, body(): pl.pallas_call(functools.partial(state_kernel, times, chans), out_shape=(...  22 us
    pallas_call x1, Pallas kernels, body(): pl.pallas_call(scale_kernel, out_shape=jax.ShapeDtypeStruct((batch, lengt...  1.88 us

profile of v8, /device:TPU:32, one launch (start us, length us, event | category | flops | bytes accessed | tf_op | source)
XLA Modules:
  0.0 23.9 jit_solution(17034559911425281884)
XLA Ops:
  0.0 22.0 %shard_map.46 = (f32[4,512,640]{2,1,0:T(8,128)S(1)}, f32[8,256]{1,0:T(8,128)S(1)}) custom-call(f32[4,512,640]{2,1,0:T(8,128)} %decay_hbm.1, bf16[4,512,640]{2,1,0:T(8,128)(2,1)} %drive_hbm.1, bf16[4,512,640]{2,1,0:T(8,128)(2,1)} %gate_hbm.1, f32[640]{0:T(1024)} %gain_hbm.1), custom_call_target="tpu_custom_call" | custom-call | tf_op jit(solution)/shard_map/pallas_call | solution.py:310
  22.0 1.9 %shard_map.47 = bf16[4,512,640]{2,1,0:T(8,128)(2,1)} custom-call(f32[4,512,640]{2,1,0:T(8,128)S(1)} %get-tuple-element.7.gated_ref, f32[8,256]{1,0:T(8,128)S(1)} %get-tuple-element.8.scale_ref), custom_call_target="tpu_custom_call" | custom-call | tf_op jit(solution)/shard_map/pallas_call | solution.py:338

commit v9 on v8

--- a/solution.py
+++ b/solution.py
@@ -36,8 +36,8 @@
 
 def state_kernel(
     times, chans, decay_hbm, drive_hbm, gate_hbm, gain_hbm, gated_ref, scale_ref,
-    decay, drives, gate, gain, logs, local, rounded, fall, lower, ends, row_buf, col_buf, power_buf,
-    load_sem, row_send, row_recv, col_send, col_recv, power_send, power_recv,
+    decay, drives, gate, gain, logs, local, rounded, fall, lower, ends, starts, row_buf, col_buf, before, hand_buf, power_buf,
+    load_sem, row_send, row_recv, hand_send, hand_recv, col_send, col_recv, power_send, power_recv,
 ):
     batch, length, width = decay_hbm.shape
     halves = length // BLOCK
@@ -73,15 +73,14 @@
     chips = COLS // CORES
     chip, core = col // CORES, lax.rem(col, CORES)
     leads = core == CORES - 1
-    row_peers = [
-        (row * COLS + lax.rem(chip + k, chips) * CORES + c, chan) for c in reversed(range(CORES)) for k in range(1, chips)
-    ]
-    row_peers += [(row * COLS + chip * CORES + lax.rem(core + k, CORES), chan) for k in range(1, CORES)]
+    lead_of = [(row * COLS + lax.rem(chip + k, chips) * CORES + CORES - 1, chan) for k in range(chips)]
+    mates = [(row * COLS + lax.rem(chip + k, chips) * CORES + c, chan) for k in range(1, chips) for c in range(CORES)]
+    mate = (row * COLS + chip * CORES + CORES - 1 - core, chan)
     col_peers = [
         (lax.rem(row + k, rows) * COLS + chip * CORES + c, chan) for k in range(1, rows) for c in range(CORES)
     ]
     chan_peers = [(time, lax.rem(chan + k, chans)) for k in range(1, chans)]
-    peers = row_peers + col_peers + chan_peers
+    peers = mates + [mate] + col_peers + chan_peers
     barrier = pltpu.get_barrier_semaphore()
     for peer in peers:
         pl.semaphore_signal(barrier, inc=1, device_id=peer, device_id_type=MESH)
@@ -123,23 +122,30 @@
         row_buf[col, b, 1:2, :] = state
 
     def start_row(b):
-        for peer in row_peers:
-            pltpu.make_async_remote_copy(
-                row_buf.at[col, b], row_buf.at[col, b], row_send, row_recv.at[b],
-                device_id=peer, device_id_type=MESH,
-            ).start()
-
-    before = {}
+        for k in range(1, chips):
+            row_copy(b, lead_of[k]).start()
+        pl.when(core == 0)(row_copy(b, lead_of[0]).start)
+
+    def row_copy(b, peer):
+        return pltpu.make_async_remote_copy(
+            row_buf.at[col, b], row_buf.at[col, b], row_send, row_recv.at[b], device_id=peer, device_id_type=MESH
+        )
+
+    def handed(b):
+        return pltpu.make_async_remote_copy(
+            hand_buf.at[b], before.at[b], hand_send, hand_recv.at[b], device_id=mate, device_id_type=MESH
+        )
 
     def send_col(b):
         several = row_buf.at[pl.ds(0, COLS - 1), b]
         pltpu.make_async_copy(several, several, row_recv.at[b]).wait()
         keep, state = one, none
-        keep_before, state_before = keep, state
+        keep_chip, state_chip, keep_before, state_before = keep, state, keep, state
         for j in range(COLS):
             keep, state = row_buf[j, b, 0:1, :] * keep, row_buf[j, b, 0:1, :] * state + row_buf[j, b, 1:2, :]
-            keep_before, state_before = jnp.where(j < col, keep, keep_before), jnp.where(j < col, state, state_before)
-        before[b] = keep_before, state_before
+            inside, earlier = j < col, j < chip * CORES
+            keep_before, state_before = jnp.where(inside, keep, keep_before), jnp.where(inside, state, state_before)
+            keep_chip, state_chip = jnp.where(earlier, keep, keep_chip), jnp.where(earlier, state, state_chip)
         col_buf[row, b, 0:1, :] = keep
         col_buf[row, b, 1:2, :] = state
         for i, peer in enumerate(col_peers):
@@ -147,9 +153,15 @@
                 col_buf.at[row, b], col_buf.at[row, b], col_send.at[i % CORES], col_recv.at[b],
                 device_id=peer, device_id_type=MESH,
             )
-            pl.when(jnp.logical_and(leads, row + i // CORES + 1 < rows))(copy.start)
+            pl.when(row + i // CORES + 1 < rows)(copy.start)
+        before[b, 0:1, :] = keep_before
+        before[b, 1:2, :] = state_before
+        hand_buf[b, 0:1, :] = keep_chip
+        hand_buf[b, 1:2, :] = state_chip
+        handed(b).start()
 
     def wait_col(b):
+        pl.when(core == 0)(handed(b).wait_recv)
         for k in range(1, rows):
             several = col_buf.at[pl.ds(0, k), b]
             pl.when(row == k)(pltpu.make_async_copy(several, several, col_recv.at[b]).wait)
@@ -158,8 +170,7 @@
         state = none
         for j in range(rows):
             state = jnp.where(j < row, col_buf[j, b, 0:1, :] * state + col_buf[j, b, 1:2, :], state)
-        keep_before, state_before = before[b]
-        return keep_before * state + state_before
+        return before[b, 0:1, :] * state + before[b, 1:2, :]
 
     def gate_block(block):
         local[block] = jnp.dot(lower[...], drives[block].reshape(2 * BLOCK, width), preferred_element_type=F32)
@@ -184,11 +195,11 @@
         start = enter(b)
         powers = jnp.zeros((halves, BLOCK), F32)
         for part in range(halves):
-            block, where = b * halves + part, part * BLOCK
+            block = b * halves + part
+            starts[block : block + 1, :] = start
             squares = []
             for here in chunks:
                 gated = logs[block, here, :] * (local[block, here, :] + start)
-                gated_ref[b, where + here.start : where + here.stop, :] = gated
                 square = gated * gated
                 square = sum(square[:, k : k + LANES] for k in range(0, width, LANES))
                 squares.append(jnp.concatenate(parts(square), axis=1))
@@ -235,11 +246,12 @@
     gains.start()
 
     spread(0)
-    for b in range(batch):
+    for b in range(batch - 1):
         gate_batch(b)
     for b in range(batch):
-        send_col(b)
-    for group in (range(2), *([b] for b in range(2, batch))):
+        pl.when(leads)(functools.partial(send_col, b))
+    gate_batch(batch - 1)
+    for group in ([b] for b in range(batch)):
         for b in group:
             wait_col(b)
         for b in group:
@@ -250,16 +262,22 @@
     gains.wait()
     by_gain = jnp.broadcast_to(gain[...].reshape(1, width), (CHUNK, width))
 
-    def weigh(i, carry):
-        here = pl.ds(pl.multiple_of(i * CHUNK, CHUNK), CHUNK)
-        for b in range(batch):
-            gated_ref[b, here, :] = gated_ref[b, here, :] * by_gain
-        return carry
-
-    lax.fori_loop(0, length // CHUNK, weigh, 0)
-
-    several = row_buf.at[pl.ds(0, COLS - 1)]
-    pltpu.make_async_copy(several, several, row_send).wait()
+    for block in range(blocks):
+        start = jnp.broadcast_to(starts[block : block + 1, :], (CHUNK, width))
+
+        def weigh(i, carry):
+            here = pl.ds(pl.multiple_of(i * CHUNK, CHUNK), CHUNK)
+            there = pl.ds(pl.multiple_of(block % halves * BLOCK + i * CHUNK, CHUNK), CHUNK)
+            gated = logs[block, here, :] * (local[block, here, :] + start)
+            gated_ref[block // halves, there, :] = gated * by_gain
+            return carry
+
+        lax.fori_loop(0, BLOCK // CHUNK, weigh, 0, unroll=2)
+
+    for c in range(CORES):
+        several = row_buf.at[pl.ds(0, chips - c)]
+        pl.when(core == c)(pltpu.make_async_copy(several, several, row_send).wait)
+    pl.when(leads)(pltpu.make_async_copy(hand_buf, hand_buf, hand_send).wait)
     for k in range(1, rows):
         several = col_buf.at[pl.ds(0, k)]
         for c in range(CORES):
@@ -323,10 +341,14 @@
                 pltpu.VMEM((BLOCK, BLOCK), BF16),
                 pltpu.VMEM((BLOCK, 2 * BLOCK), BF16),
                 pltpu.VMEM((2 * blocks, width), F32),
+                pltpu.VMEM((blocks, width), F32),
                 pltpu.VMEM((COLS, batch, 2, width), F32),
                 pltpu.VMEM((rows, batch, 2, width), F32),
+                pltpu.VMEM((batch, 2, width), F32),
+                pltpu.VMEM((batch, 2, width), F32),
                 pltpu.VMEM((chans, batch, length // BLOCK, BLOCK), F32),
                 dma((blocks + 3,)),
+                dma, dma((batch,)),
                 dma, dma((batch,)),
                 dma((CORES,)), dma((batch,)),
                 dma, dma,

time: 24 us -> 23.9 us (level)
  no operation moved by 1% of the time
where the time goes in v9:
time: 23.9 us; the launch traced here: 23.8 us
  Pallas kernels  23.8 us (100%)
    pallas_call x1, Pallas kernels, body(): pl.pallas_call(functools.partial(state_kernel, times, chans), out_shape=(...  21.9 us
    pallas_call x1, Pallas kernels, body(): pl.pallas_call(scale_kernel, out_shape=jax.ShapeDtypeStruct((batch, lengt...  1.88 us

profile of v9, /device:TPU:32, one launch (start us, length us, event | category | flops | bytes accessed | tf_op | source)
XLA Modules:
  0.0 23.8 jit_solution(16567160428445831217)
XLA Ops:
  0.0 21.9 %shard_map.46 = (f32[4,512,640]{2,1,0:T(8,128)S(1)}, f32[8,256]{1,0:T(8,128)S(1)}) custom-call(f32[4,512,640]{2,1,0:T(8,128)} %decay_hbm.1, bf16[4,512,640]{2,1,0:T(8,128)(2,1)} %drive_hbm.1, bf16[4,512,640]{2,1,0:T(8,128)(2,1)} %gate_hbm.1, f32[640]{0:T(1024)} %gain_hbm.1), custom_call_target="tpu_custom_call" | custom-call | tf_op jit(solution)/shard_map/pallas_call | solution.py:328
  21.9 1.9 %shard_map.47 = bf16[4,512,640]{2,1,0:T(8,128)(2,1)} custom-call(f32[4,512,640]{2,1,0:T(8,128)S(1)} %get-tuple-element.7.gated_ref, f32[8,256]{1,0:T(8,128)S(1)} %get-tuple-element.8.scale_ref), custom_call_target="tpu_custom_call" | custom-call | tf_op jit(solution)/shard_map/pallas_call | solution.py:360

commit v10 on v9

--- a/solution.py
+++ b/solution.py
@@ -34,9 +34,28 @@
     return high, (x - high.astype(F32)).astype(BF16)
 
 
+def spread_rows(scale):
+    rows = jnp.concatenate([scale, jnp.zeros((8 - scale.shape[0], BLOCK), F32)], axis=0)
+    wide = (16, scale.shape[0] * LANES)
+    pick = jnp.where(lax.rem(iota(wide, 0), 8) == iota(wide, 1) // LANES, 1.0, 0.0).astype(BF16)
+    return lax.dot_general(jnp.concatenate(parts(rows), axis=0), pick, TN, preferred_element_type=F32)
+
+
+def scale_block(part, gated, factors, store):
+    width = gated.shape[-1]
+
+    def scale_chunk(i, carry):
+        here = pl.ds(pl.multiple_of(i * CHUNK, CHUNK), CHUNK)
+        factor = jnp.concatenate([factors[here, part * LANES : (part + 1) * LANES]] * (width // LANES), axis=1)
+        store(i, (gated[here, :] * factor).astype(BF16))
+        return carry
+
+    lax.fori_loop(0, BLOCK // CHUNK, scale_chunk, 0, unroll=4)
+
+
 def state_kernel(
-    times, chans, decay_hbm, drive_hbm, gate_hbm, gain_hbm, gated_ref, scale_ref,
-    decay, drives, gate, gain, logs, local, rounded, fall, lower, ends, starts, row_buf, col_buf, before, hand_buf, power_buf,
+    times, chans, decay_hbm, drive_hbm, gate_hbm, gain_hbm, result_ref, gated_ref, scale_ref,
+    decay, drives, gate, gain, logs, local, rounded, fall, lower, ends, starts, factors, row_buf, col_buf, before, hand_buf, power_buf,
     load_sem, row_send, row_recv, hand_send, hand_recv, col_send, col_recv, power_send, power_recv,
 ):
     batch, length, width = decay_hbm.shape
@@ -214,7 +233,7 @@
     def send_power(b):
         for peer in chan_peers:
             pltpu.make_async_remote_copy(
-                power_buf.at[chan, b], power_buf.at[chan, b], power_send, power_recv,
+                power_buf.at[chan, b], power_buf.at[chan, b], power_send, power_recv.at[b],
                 device_id=peer, device_id_type=MESH,
             ).start()
 
@@ -267,9 +286,11 @@
 
         def weigh(i, carry):
             here = pl.ds(pl.multiple_of(i * CHUNK, CHUNK), CHUNK)
-            there = pl.ds(pl.multiple_of(block % halves * BLOCK + i * CHUNK, CHUNK), CHUNK)
             gated = logs[block, here, :] * (local[block, here, :] + start)
-            gated_ref[block // halves, there, :] = gated * by_gain
+            if block < blocks - halves:
+                decay[block, here, :] = gated * by_gain
+            else:
+                gated_ref[block - blocks + halves, here, :] = gated * by_gain
             return carry
 
         lax.fori_loop(0, BLOCK // CHUNK, weigh, 0, unroll=2)
@@ -285,35 +306,44 @@
             pl.when(jnp.logical_and(leads, row + k + 1 == rows))(copy.wait)
     several = power_buf.at[pl.ds(0, chans - 1)]
     pltpu.make_async_copy(several, several, power_send).wait()
-    pltpu.make_async_copy(several, several, power_recv).wait()
-    for b in range(batch):
+
+    def scale_of(b):
+        several = power_buf.at[pl.ds(0, chans - 1), b]
+        pltpu.make_async_copy(several, several, power_recv.at[b]).wait()
         power = sum(power_buf[j, b] for j in range(chans)) * (half * half / (width * chans))
-        scale_ref[b * halves : (b + 1) * halves, :] = half * lax.rsqrt(power + 1e-06)
-
-
-def scale_kernel(gated_ref, scale_ref, out_hbm, result, factors, sem):
-    batch, length, width = result.shape
-    blocks = scale_ref.shape[0]
-    halves = blocks // batch
-    wide = (2 * blocks, blocks * LANES)
-    pick = jnp.where(lax.rem(iota(wide, 0), blocks) == iota(wide, 1) // LANES, 1.0, 0.0).astype(BF16)
-    factors[...] = lax.dot_general(
-        jnp.concatenate(parts(scale_ref[...]), axis=0), pick, TN, preferred_element_type=F32
-    )
-
-    def write(block, carry):
-        b, where = block // halves, lax.rem(block, halves) * BLOCK
-        lane = pl.ds(pl.multiple_of(block * LANES, LANES), LANES)
-        for k in range(0, BLOCK, CHUNK):
-            here = pl.ds(pl.multiple_of(where + k, CHUNK), CHUNK)
-            factor = jnp.concatenate([factors[k : k + CHUNK, lane]] * (width // LANES), axis=1)
-            result[b, here, :] = (gated_ref[b, here, :] * factor).astype(result.dtype)
-        there = (b, pl.ds(pl.multiple_of(where, BLOCK), BLOCK))
-        pltpu.make_async_copy(result.at[there], out_hbm.at[there], sem).start()
-        return carry
-
-    lax.fori_loop(0, blocks, write, 0)
-    pltpu.make_async_copy(result, out_hbm, sem).wait()
+        return half * lax.rsqrt(power + 1e-06)
+
+    for b in range(batch - 1):
+        factors[...] = spread_rows(scale_of(b))
+        for part in range(halves):
+
+            def store(i, value):
+                where = pl.multiple_of(part * BLOCK + i * CHUNK, CHUNK)
+                result_ref[b, pl.ds(where, CHUNK), :] = value
+
+            scale_block(part, decay.at[b * halves + part], factors, store)
+    scale_ref[...] = scale_of(batch - 1)
+
+
+def scale_kernel(result_ref, gated_ref, scale_ref, out_hbm, last, factors, sem):
+    done, halves = result_ref.shape[0], gated_ref.shape[0]
+
+    def at(b, part):
+        return b, pl.ds(part * BLOCK, BLOCK)
+
+    for b in range(done):
+        for part in range(halves):
+            pltpu.make_async_copy(result_ref.at[at(b, part)], out_hbm.at[at(b, part)], sem).start()
+    factors[...] = spread_rows(scale_ref[...])
+    for part in range(halves):
+
+        def store(i, value):
+            where = pl.multiple_of(part * BLOCK + i * CHUNK, CHUNK)
+            last[0, pl.ds(where, CHUNK), :] = value
+
+        scale_block(part, gated_ref.at[part], factors, store)
+        pltpu.make_async_copy(last.at[at(0, part)], out_hbm.at[at(done, part)], sem).start()
+    pltpu.make_async_copy(out_hbm, out_hbm, sem).wait()
 
 
 def solution(mesh):
@@ -325,11 +355,16 @@
         rows = times // COLS
         dma = pltpu.SemaphoreType.DMA
         vmem = pl.BlockSpec(memory_space=pltpu.VMEM)
-        gated, scale = pl.pallas_call(
+        halves = length // BLOCK
+        staged = pl.pallas_call(
             functools.partial(state_kernel, times, chans),
-            out_shape=(pltpu.VMEM((batch, length, width), F32), pltpu.VMEM((blocks, BLOCK), F32)),
+            out_shape=(
+                pltpu.VMEM((batch - 1, length, width), BF16),
+                pltpu.VMEM((halves, BLOCK, width), F32),
+                pltpu.VMEM((halves, BLOCK), F32),
+            ),
             in_specs=[pl.BlockSpec(memory_space=pltpu.HBM)] * 4,
-            out_specs=(vmem, vmem),
+            out_specs=(vmem, vmem, vmem),
             scratch_shapes=[
                 pltpu.VMEM((blocks, BLOCK, width), F32),
                 pltpu.VMEM((blocks, 2, BLOCK, width), BF16),
@@ -342,6 +377,7 @@
                 pltpu.VMEM((BLOCK, 2 * BLOCK), BF16),
                 pltpu.VMEM((2 * blocks, width), F32),
                 pltpu.VMEM((blocks, width), F32),
+                pltpu.VMEM((BLOCK, halves * LANES), F32),
                 pltpu.VMEM((COLS, batch, 2, width), F32),
                 pltpu.VMEM((rows, batch, 2, width), F32),
                 pltpu.VMEM((batch, 2, width), F32),
@@ -351,7 +387,7 @@
                 dma, dma((batch,)),
                 dma, dma((batch,)),
                 dma((CORES,)), dma((batch,)),
-                dma, dma,
+                dma, dma((batch,)),
             ],
             compiler_params=pltpu.CompilerParams(
                 collective_id=0, has_side_effects=True, vmem_limit_bytes=57 * 2**20
@@ -360,15 +396,15 @@
         return pl.pallas_call(
             scale_kernel,
             out_shape=jax.ShapeDtypeStruct((batch, length, width), BF16),
-            in_specs=[vmem, vmem],
+            in_specs=[vmem, vmem, vmem],
             out_specs=pl.BlockSpec(memory_space=pltpu.HBM),
             scratch_shapes=[
-                pltpu.VMEM((batch, length, width), BF16),
-                pltpu.VMEM((BLOCK, blocks * LANES), F32),
+                pltpu.VMEM((1, length, width), BF16),
+                pltpu.VMEM((BLOCK, halves * LANES), F32),
                 dma,
             ],
             compiler_params=pltpu.CompilerParams(vmem_limit_bytes=16 * 2**20),
-        )(gated, scale)
+        )(*staged)
 
     in_specs = (P(None, "time", "chan"), P(None, "time", "chan"), P(None, "time", "chan"), P("chan"))
     return jax.shard_map(body, mesh=mesh, in_specs=in_specs, out_specs=P(None, "time", "chan"), check_vma=False)

time: 23.9 us -> 23.5 us (0.983)
  Pallas kernels: 23.8 us -> 23.4 us
    pallas_call x1, Pallas kernels: 1.88 us -> 1.49 us  [body(): pl.pallas_call(scale_kernel, out_shape=jax.ShapeDtypeStruct((batch, lengt...]
where the time goes in v10:
time: 23.5 us; the launch traced here: 23.4 us
  Pallas kernels  23.4 us (100%)
    pallas_call x1, Pallas kernels, body(): pl.pallas_call(functools.partial(state_kernel, times, chans), out_shape=(...  22 us
    pallas_call x1, Pallas kernels, body(): pl.pallas_call(scale_kernel, out_shape=jax.ShapeDtypeStruct((batch, lengt...  1.49 us

profile of v10, /device:TPU:32, one launch (start us, length us, event | category | flops | bytes accessed | tf_op | source)
XLA Modules:
  0.0 23.4 jit_solution(7507484364948166619)
XLA Ops:
  0.0 22.0 %shard_map.46 = (bf16[3,512,640]{2,1,0:T(8,128)(2,1)S(1)}, f32[2,256,640]{2,1,0:T(8,128)S(1)}, f32[2,256]{1,0:T(2,128)S(1)}) custom-call(f32[4,512,640]{2,1,0:T(8,128)} %decay_hbm.1, bf16[4,512,640]{2,1,0:T(8,128)(2,1)} %drive_hbm.1, bf16[4,512,640]{2,1,0:T(8,128)(2,1)} %gate_hbm.1, f32[640]{0:T(1024)} %gain_hbm.1), custom_call_target="tpu_custom_call" | custom-call | tf_op jit(solution)/shard_map/pallas_call | solution.py:359
  22.0 1.5 %shard_map.47 = bf16[4,512,640]{2,1,0:T(8,128)(2,1)} custom-call(bf16[3,512,640]{2,1,0:T(8,128)(2,1)S(1)} %get-tuple-element.8.result_ref, f32[2,256,640]{2,1,0:T(8,128)S(1)} %get-tuple-element.9.gated_ref, f32[2,256]{1,0:T(2,128)S(1)} %get-tuple-element.10.scale_ref), custom_call_target="tpu_custom_call" | custom-call | tf_op jit(solution)/shard_map/pallas_call | solution.py:396

commit v11 on v10

--- a/solution.py
+++ b/solution.py
@@ -253,11 +253,9 @@
         if block % halves == halves - 1 and block + 1 < blocks:
             b = block // halves
             send_row(b)
-            if b == 1:
+            if b == 0:
                 pl.semaphore_wait(barrier, len(peers))
-                start_row(0)
-            if b >= 1:
-                start_row(b)
+            start_row(b)
     send_row(batch - 1)
     start_row(batch - 1)
     for copy in gates[blocks // 2 :]:
@@ -265,9 +263,11 @@
     gains.start()
 
     spread(0)
-    for b in range(batch - 1):
+    for b in range(batch - 2):
         gate_batch(b)
-    for b in range(batch):
+    pl.when(leads)(functools.partial(send_col, 0))
+    gate_batch(batch - 2)
+    for b in range(1, batch):
         pl.when(leads)(functools.partial(send_col, b))
     gate_batch(batch - 1)
     for group in ([b] for b in range(batch)):

time: 23.5 us -> 23.4 us (level)
  no operation moved by 1% of the time
where the time goes in v11:
time: 23.4 us; the launch traced here: 23.3 us
  Pallas kernels  23.3 us (100%)
    pallas_call x1, Pallas kernels, body(): pl.pallas_call(functools.partial(state_kernel, times, chans), out_shape=(...  21.8 us
    pallas_call x1, Pallas kernels, body(): pl.pallas_call(scale_kernel, out_shape=jax.ShapeDtypeStruct((batch, lengt...  1.49 us

profile of v11, /device:TPU:32, one launch (start us, length us, event | category | flops | bytes accessed | tf_op | source)
XLA Modules:
  0.0 23.3 jit_solution(8543626866673914203)
XLA Ops:
  0.0 21.8 %shard_map.46 = (bf16[3,512,640]{2,1,0:T(8,128)(2,1)S(1)}, f32[2,256,640]{2,1,0:T(8,128)S(1)}, f32[2,256]{1,0:T(2,128)S(1)}) custom-call(f32[4,512,640]{2,1,0:T(8,128)} %decay_hbm.1, bf16[4,512,640]{2,1,0:T(8,128)(2,1)} %drive_hbm.1, bf16[4,512,640]{2,1,0:T(8,128)(2,1)} %gate_hbm.1, f32[640]{0:T(1024)} %gain_hbm.1), custom_call_target="tpu_custom_call" | custom-call | tf_op jit(solution)/shard_map/pallas_call | solution.py:359
  21.8 1.5 %shard_map.47 = bf16[4,512,640]{2,1,0:T(8,128)(2,1)} custom-call(bf16[3,512,640]{2,1,0:T(8,128)(2,1)S(1)} %get-tuple-element.8.result_ref, f32[2,256,640]{2,1,0:T(8,128)S(1)} %get-tuple-element.9.gated_ref, f32[2,256]{1,0:T(2,128)S(1)} %get-tuple-element.10.scale_ref), custom_call_target="tpu_custom_call" | custom-call | tf_op jit(solution)/shard_map/pallas_call | solution.py:396

commit v12 on v10

--- a/solution.py
+++ b/solution.py
@@ -56,7 +56,7 @@
 def state_kernel(
     times, chans, decay_hbm, drive_hbm, gate_hbm, gain_hbm, result_ref, gated_ref, scale_ref,
     decay, drives, gate, gain, logs, local, rounded, fall, lower, ends, starts, factors, row_buf, col_buf, before, hand_buf, power_buf,
-    load_sem, row_send, row_recv, hand_send, hand_recv, col_send, col_recv, power_send, power_recv,
+    load_sem, row_send, row_recv, hand_send, col_send, col_recv, power_send, power_recv,
 ):
     batch, length, width = decay_hbm.shape
     halves = length // BLOCK
@@ -81,7 +81,7 @@
     decays = [load(at(decay_hbm, k), decay.at[k], k) for k in range(blocks)]
     driving = [load(at(drive_hbm, k), drives.at[k, 0], k + 2) for k in range(blocks)]
     gates = [load(at(gate_hbm, k), gate.at[k], k // halves) for k in range(blocks)]
-    gains = load(gain_hbm, gain, blocks + 2)
+    gains = load(gain_hbm, gain, blocks // 2)
     decays[0].start()
     decays[1].start()
     for k in range(blocks):
@@ -98,7 +98,7 @@
     col_peers = [
         (lax.rem(row + k, rows) * COLS + chip * CORES + c, chan) for k in range(1, rows) for c in range(CORES)
     ]
-    chan_peers = [(time, lax.rem(chan + k, chans)) for k in range(1, chans)]
+    chan_peers = [(time, lax.rem(chan + k, chans)) for k in sorted(range(1, chans), key=lambda k: -min(k, chans - k))]
     peers = mates + [mate] + col_peers + chan_peers
     barrier = pltpu.get_barrier_semaphore()
     for peer in peers:
@@ -152,7 +152,7 @@
 
     def handed(b):
         return pltpu.make_async_remote_copy(
-            hand_buf.at[b], before.at[b], hand_send, hand_recv.at[b], device_id=mate, device_id_type=MESH
+            hand_buf.at[b], before.at[b], hand_send, col_recv.at[b], device_id=mate, device_id_type=MESH
         )
 
     def send_col(b):
@@ -180,10 +180,10 @@
         handed(b).start()
 
     def wait_col(b):
-        pl.when(core == 0)(handed(b).wait_recv)
-        for k in range(1, rows):
+        for k in range(1, rows + 1):
             several = col_buf.at[pl.ds(0, k), b]
-            pl.when(row == k)(pltpu.make_async_copy(several, several, col_recv.at[b]).wait)
+            copy = pltpu.make_async_copy(several, several, col_recv.at[b])
+            pl.when(row + (core == 0).astype(jnp.int32) == k)(copy.wait)
 
     def enter(b):
         state = none
@@ -383,9 +383,9 @@
                 pltpu.VMEM((batch, 2, width), F32),
                 pltpu.VMEM((batch, 2, width), F32),
                 pltpu.VMEM((chans, batch, length // BLOCK, BLOCK), F32),
-                dma((blocks + 3,)),
+                dma((blocks + 2,)),
                 dma, dma((batch,)),
-                dma, dma((batch,)),
+                dma,
                 dma((CORES,)), dma((batch,)),
                 dma, dma((batch,)),
             ],

time: 23.5 us -> 23.5 us (level)
  no operation moved by 1% of the time
where the time goes in v12:
time: 23.5 us; the launch traced here: 23.4 us
  Pallas kernels  23.4 us (100%)
    pallas_call x1, Pallas kernels, body(): pl.pallas_call(functools.partial(state_kernel, times, chans), out_shape=(...  21.9 us
    pallas_call x1, Pallas kernels, body(): pl.pallas_call(scale_kernel, out_shape=jax.ShapeDtypeStruct((batch, lengt...  1.49 us

profile of v12, /device:TPU:32, one launch (start us, length us, event | category | flops | bytes accessed | tf_op | source)
XLA Modules:
  0.0 23.4 jit_solution(13694156791704025084)
XLA Ops:
  0.0 21.9 %shard_map.46 = (bf16[3,512,640]{2,1,0:T(8,128)(2,1)S(1)}, f32[2,256,640]{2,1,0:T(8,128)S(1)}, f32[2,256]{1,0:T(2,128)S(1)}) custom-call(f32[4,512,640]{2,1,0:T(8,128)} %decay_hbm.1, bf16[4,512,640]{2,1,0:T(8,128)(2,1)} %drive_hbm.1, bf16[4,512,640]{2,1,0:T(8,128)(2,1)} %gate_hbm.1, f32[640]{0:T(1024)} %gain_hbm.1), custom_call_target="tpu_custom_call" | custom-call | tf_op jit(solution)/shard_map/pallas_call | solution.py:359
  21.9 1.5 %shard_map.47 = bf16[4,512,640]{2,1,0:T(8,128)(2,1)} custom-call(bf16[3,512,640]{2,1,0:T(8,128)(2,1)S(1)} %get-tuple-element.8.result_ref, f32[2,256,640]{2,1,0:T(8,128)S(1)} %get-tuple-element.9.gated_ref, f32[2,256]{1,0:T(2,128)S(1)} %get-tuple-element.10.scale_ref), custom_call_target="tpu_custom_call" | custom-call | tf_op jit(solution)/shard_map/pallas_call | solution.py:396

commit v13 on v10

--- a/solution.py
+++ b/solution.py
@@ -244,9 +244,6 @@
     prepare(1)
     for block in range(blocks):
         wait_pair(block + 2, 3 if block + 2 < blocks else 1)
-        if block == blocks // 2:
-            for copy in gates[: blocks // 2]:
-                copy.start()
         mixed(block)
         if block + 2 < blocks:
             prepare(block + 2)
@@ -260,7 +257,7 @@
                 start_row(b)
     send_row(batch - 1)
     start_row(batch - 1)
-    for copy in gates[blocks // 2 :]:
+    for copy in gates:
         copy.start()
     gains.start()
 

time: 23.5 us -> 23.5 us (level)
  no operation moved by 1% of the time
where the time goes in v13:
time: 23.5 us; the launch traced here: 23.4 us
  Pallas kernels  23.4 us (100%)
    pallas_call x1, Pallas kernels, body(): pl.pallas_call(functools.partial(state_kernel, times, chans), out_shape=(...  22 us
    pallas_call x1, Pallas kernels, body(): pl.pallas_call(scale_kernel, out_shape=jax.ShapeDtypeStruct((batch, lengt...  1.49 us

profile of v13, /device:TPU:32, one launch (start us, length us, event | category | flops | bytes accessed | tf_op | source)
XLA Modules:
  0.0 23.4 jit_solution(6801075301427903693)
XLA Ops:
  0.0 22.0 %shard_map.46 = (bf16[3,512,640]{2,1,0:T(8,128)(2,1)S(1)}, f32[2,256,640]{2,1,0:T(8,128)S(1)}, f32[2,256]{1,0:T(2,128)S(1)}) custom-call(f32[4,512,640]{2,1,0:T(8,128)} %decay_hbm.1, bf16[4,512,640]{2,1,0:T(8,128)(2,1)} %drive_hbm.1, bf16[4,512,640]{2,1,0:T(8,128)(2,1)} %gate_hbm.1, f32[640]{0:T(1024)} %gain_hbm.1), custom_call_target="tpu_custom_call" | custom-call | tf_op jit(solution)/shard_map/pallas_call | solution.py:356
  22.0 1.5 %shard_map.47 = bf16[4,512,640]{2,1,0:T(8,128)(2,1)} custom-call(bf16[3,512,640]{2,1,0:T(8,128)(2,1)S(1)} %get-tuple-element.8.result_ref, f32[2,256,640]{2,1,0:T(8,128)S(1)} %get-tuple-element.9.gated_ref, f32[2,256]{1,0:T(2,128)S(1)} %get-tuple-element.10.scale_ref), custom_call_target="tpu_custom_call" | custom-call | tf_op jit(solution)/shard_map/pallas_call | solution.py:393
